TPU v7x, 256 devices: a whole 4x4x8 slice. The times are simulated.
256 devices in a mesh: chan: 4 (over y), slab: 64 (over x, z, core).
Axes of the slice: x: 4, y: 4, z: 8, core: 2. Of those that a mesh axis runs over, the one named last changes fastest.
Arguments:
- flux: float32 [4, 4096, 128], P('chan', 'slab'), may hold values from -6 to 6
- offsets: int32 [4096, 128], P('slab'), may hold values from 0 to 8191
- counts: int32 [4096], P('slab'), may hold values from 96 to 128
- dest_owner: int32 [4096, 1], P('slab'), may hold values from 0 to 63; in each aligned block of 64 rows (0 to 63, 64 to 127, ...) at most 2 rows name the same one
- dest_tile: int32 [4096], P('slab'), may hold values from 0 to 31
- dirty: float32 [4, 4096, 4096], P('chan', 'slab'), may hold values from -60 to 60
- psf_real: float32 [4, 8192, 8192], P('chan', None, 'slab'), may hold values from -96 to 96
- psf_imag: float32 [4, 8192, 8192], P('chan', None, 'slab'), may hold values from -96 to 96
Outputs:
- residual: float32 [4, 4096, 4096], P('chan', 'slab')
- rms_values: float32 [4], replicated
- peak_values: float32 [4], replicated
Inputs may be any that keep to these rules, and one draw needn't show every extreme that they name: `dest_owner`: among the 64 blocks of one device (aligned blocks of rows) at most 2 name the same owner, a bound that some device reaches. `counts`: slots at or beyond a block's count hold no component.
All inputs are finite; a program needn't handle non-finite values.
Results may differ from a plain program's by a relative error of at most 0.00005.
Values sent between devices are 32-bit elements; how exact they have to be, the bound alone decides.
No kernel may reach another device: no remote copies, remote signals or barrier semaphores. Data moves between devices by JAX's collectives and lax.ppermute only.
A program may use at most 128 MiB of HBM per device.

v0:
```python
import math

import jax
import jax.numpy as jnp
from jax import lax
from jax.sharding import Mesh
from jax.sharding import PartitionSpec as P

TILE_R = 64
TILE_C = 128
SLAB = ("slab_0", "slab_1", "slab_2")


PRECISE = lax.Precision.HIGHEST


def cut_along(shard, dim, peers):
    before, after = (shard.shape[:dim], shard.shape[dim + 1 :])
    return jnp.moveaxis(shard.reshape(*before, peers, -1, *after), dim, 0)


def joined_along(pieces, dim):
    pieces = jnp.moveaxis(pieces, 0, dim)
    shape = pieces.shape
    return pieces.reshape(*shape[:dim], shape[dim] * shape[dim + 1], *shape[dim + 2 :])


def turned_blocks(pieces, axes, sequence):
    shape = [lax.axis_size(a) for a in axes]
    pieces = pieces.reshape(*shape, *pieces.shape[1:])
    for k in sequence:
        pieces = lax.all_to_all(pieces, axes[k], split_axis=k, concat_axis=k, tiled=True)
    return pieces.reshape(-1, *pieces.shape[len(axes) :])


def core_and_chips(shard, groups, sequence, split_dim, concat_dim):
    peers = lax.axis_size(groups[0]) * lax.axis_size(groups[1])
    pieces = cut_along(shard, split_dim, peers)
    return joined_along(turned_blocks(pieces, groups, sequence), concat_dim)


def sent_to_all(shard, axis):
    copies = jnp.broadcast_to(shard, (lax.axis_size(axis), *shard.shape))
    return lax.all_to_all(copies, axis, split_axis=0, concat_axis=0, tiled=True)


def taken_together(shard, axis):
    everything = sent_to_all(shard, axis)
    return jnp.sum(everything, axis=0)


def over_copies(shard, axis):
    everything = sent_to_all(shard, axis)
    return jnp.max(everything, axis=0)


def rows_first(arrays, axis, dims):
    turned = [jnp.moveaxis(a, dim, 0) for a, dim in zip(arrays, dims)]
    widths = [t[0].size for t in turned]
    both = jnp.concatenate([t.reshape(-1, w) for t, w in zip(turned, widths)], axis=1)
    whole = lax.all_gather(both, axis, axis=0, tiled=True)
    pieces = jnp.split(whole, [sum(widths[:k]) for k in range(1, len(widths))], axis=1)
    return tuple(
        (
            jnp.moveaxis(b.reshape(-1, *t.shape[1:]), 0, dim)
            for b, t, dim in zip(pieces, turned, dims)
        )
    )


def factor(length):
    levels = length.bit_length() - 1
    outer_len = 2 ** ((levels + 1) // 2)
    return (outer_len, length // outer_len)


def rotation(count_one, count_two, length, sign):
    row_ids = jnp.arange(count_one, dtype=jnp.int32)[:, None]
    col_ids = jnp.arange(count_two, dtype=jnp.int32)[None, :]
    turn_count = row_ids * col_ids % length
    angles = turn_count.astype(jnp.float32) * (2.0 * math.pi / length)
    return (jnp.cos(angles), sign * jnp.sin(angles))


def table(count_one, count_two, length, sign):
    cosine, sine = rotation(count_one, count_two, length, sign)
    first = jnp.stack([cosine, sine], axis=1)
    second = jnp.stack([-sine, cosine], axis=1)
    return jnp.stack([first, second], axis=0)


def contract(pattern, first_op, second_op):
    return jnp.einsum(pattern, first_op, second_op, precision=PRECISE)


def twiddle(values, phases):
    phase_re, phase_im = phases
    value_re = values[0]
    value_im = values[1]
    return jnp.stack(
        [value_re * phase_re - value_im * phase_im, value_re * phase_im + value_im * phase_re]
    )


def widen(phases):
    return (phases[0][:, :, None], phases[1][:, :, None])


def forward_rows(image, length):
    outer_len, inner_len = factor(length)
    row_count = image.shape[0]
    pieces = image.reshape(row_count, outer_len // 2, inner_len)
    partial_sum = contract(
        "rab,atk->trkb", pieces, table(outer_len // 2, outer_len, outer_len, -1.0)[0]
    )
    partial_sum = twiddle(partial_sum, rotation(outer_len, inner_len, length, -1.0))
    result = contract("srkb,sbtj->trjk", partial_sum, table(inner_len, inner_len, inner_len, -1.0))
    return result.reshape(2, row_count, length)


def forward_cols(values, length):
    outer_len, inner_len = factor(length)
    col_count = values.shape[2]
    pieces = values.reshape(2, outer_len // 2, inner_len, col_count)
    partial_sum = contract(
        "sabc,satk->tkbc", pieces, table(outer_len // 2, outer_len, outer_len, -1.0)
    )
    partial_sum = twiddle(partial_sum, widen(rotation(outer_len, inner_len, length, -1.0)))
    result = contract("skbc,sbtj->tjkc", partial_sum, table(inner_len, inner_len, inner_len, -1.0))
    return result.reshape(2, length, col_count)


def inverse_cols(values, length):
    outer_len, inner_len = factor(length)
    col_count = values.shape[2]
    pieces = values.reshape(2, outer_len, inner_len, col_count)
    partial_sum = contract("sabc,sate->tebc", pieces, table(outer_len, outer_len, outer_len, 1.0))
    partial_sum = twiddle(partial_sum, widen(rotation(outer_len, inner_len, length, 1.0)))
    result = contract(
        "sebc,sbtd->tdec", partial_sum, table(inner_len, inner_len // 2, inner_len, 1.0)
    )
    return result.reshape(2, length // 2, col_count) * (1.0 / length)


def inverse_rows(values, length):
    outer_len, inner_len = factor(length)
    row_count = values.shape[1]
    pieces = values.reshape(2, row_count, outer_len, inner_len)
    partial_sum = contract("srab,sate->treb", pieces, table(outer_len, outer_len, outer_len, 1.0))
    partial_sum = twiddle(partial_sum, rotation(outer_len, inner_len, length, 1.0))
    real_table = table(inner_len, inner_len // 2, inner_len, 1.0)[:, :, 0]
    real_part = contract("sreb,sbd->rde", partial_sum, real_table)
    return real_part.reshape(row_count, length // 2) * (1.0 / length)


def on_device(flux, offsets, counts, dest_owner, dest_tile, dirty, psf_real, psf_imag):
    slab_count = lax.axis_size(SLAB)
    chan_local, rows_dev, row_width = dirty.shape
    length = 2 * row_width
    blocks, comp_slots = offsets.shape
    slab_area = rows_dev * row_width
    across = row_width // TILE_C
    tile_row = dest_tile // across
    tile_col = dest_tile % across
    pixels = (
        (tile_row[:, None] * TILE_R + offsets // TILE_C) * row_width
        + tile_col[:, None] * TILE_C
        + offsets % TILE_C
    )
    live_mask = jnp.arange(comp_slots, dtype=jnp.int32)[None, :] < counts[:, None]
    weights = jnp.where(live_mask[None], flux, 0.0)
    owner_ids = dest_owner[:, 0]
    send_slots = 2 * blocks // slab_count
    owner_marks = (owner_ids[:, None] == jnp.arange(slab_count, dtype=jnp.int32)[None, :]).astype(
        jnp.int32
    )
    owner_ranks = jnp.sum((jnp.cumsum(owner_marks, axis=0) - 1) * owner_marks, axis=1)
    slot_index = owner_ids * send_slots + owner_ranks
    pixel_box = (
        jnp.zeros((slab_count * send_slots, comp_slots), jnp.int32).at[slot_index].set(pixels)
    )
    flux_box = (
        jnp.zeros((chan_local, slab_count * send_slots, comp_slots), jnp.float32)
        .at[:, slot_index]
        .set(weights)
    )
    got_pixels = lax.all_to_all(
        pixel_box.reshape(slab_count, send_slots, comp_slots),
        SLAB,
        split_axis=0,
        concat_axis=0,
        tiled=True,
    )
    got_flux = lax.all_to_all(
        flux_box.reshape(chan_local, slab_count, send_slots, comp_slots),
        SLAB,
        split_axis=1,
        concat_axis=1,
        tiled=True,
    )
    targets = got_pixels.reshape(-1)
    amounts = got_flux.reshape(chan_local, -1)
    raster = jnp.zeros((chan_local, slab_area), jnp.float32).at[:, targets].add(amounts)
    row_spectra = forward_rows(raster[0].reshape(rows_dev, row_width), length)
    columns = core_and_chips(row_spectra, (("slab_0", "slab_1"), "slab_2"), (1, 0), 2, 1)
    spectrum = forward_cols(columns, length)
    filtered = twiddle(spectrum, (psf_real[0], psf_imag[0]))
    narrowed = inverse_cols(filtered, length)
    returned = lax.all_to_all(narrowed, SLAB, split_axis=1, concat_axis=2, tiled=True)
    smeared = inverse_rows(returned, length)
    convolved = [dirty[0] - smeared]
    residual = jnp.stack(convolved)
    squares = jnp.sum(residual * residual, axis=(1, 2))
    peaks = jnp.max(jnp.abs(residual), axis=(1, 2))
    pixel_total = rows_dev * slab_count * row_width
    totals = taken_together(squares, SLAB)
    highest = over_copies(peaks, SLAB)
    rms_values, peak_values = rows_first((jnp.sqrt(totals / pixel_total), highest), "chan", (0, 0))
    return (residual, rms_values, peak_values)


def solution(mesh):
    torus = Mesh(
        mesh.devices.reshape(mesh.shape["chan"], 4, 8, 2), ("chan", "slab_0", "slab_1", "slab_2")
    )
    in_specs = (
        P("chan", SLAB, None),
        P(SLAB, None),
        P(SLAB),
        P(SLAB, None),
        P(SLAB),
        P("chan", SLAB, None),
        P("chan", None, SLAB),
        P("chan", None, SLAB),
    )
    out_specs = (P("chan", SLAB, None), P(), P())
    return jax.shard_map(
        on_device, mesh=torus, in_specs=in_specs, out_specs=out_specs, check_vma=False
    )
```

profile of v0, /device:TPU:1, one launch (start us, length us, event | category | flops | bytes accessed | tf_op | source)
XLA Modules:
  0.0 536.5 jit_solution(17369215564055994624)
XLA Ops:
  0.6 0.7 fusion.81
  1.4 0.1 reduce_window_sum.11
  1.5 0.8 select_reduce_fusion
  2.3 0.7 fusion.126
  3.0 0.7 fusion.127
  3.6 1.6 scatter_custom_fusion
  5.3 13.0 %all-to-all-start = ((s32[64,2,128]{2,1,0:T(2,128)}), s32[64,2,128]{2,1,0:T(2,128)S(1)}, u32[]{:S(2)}, u32[]{:S(2)}) async-start(s32[64,2,128]{2,1,0:T(2,128)} %bitcast.27), calls=%async_computation | async-start | bytes 131072 | tf_op jit(solution)/shard_map/all_to_all | solution.py:187
  18.2 0.1 sine_multiply_fusion
  18.4 0.1 broadcast_multiply_fusion
  18.5 0.1 sine_multiply_fusion.1
  18.7 0.1 fusion.120
  18.8 1.6 scatter_custom_fusion.1
  20.5 7.6 %all-to-all-done = s32[64,2,128]{2,1,0:T(2,128)S(1)} async-done(((s32[64,2,128]{2,1,0:T(2,128)}), s32[64,2,128]{2,1,0:T(2,128)S(1)}, u32[]{:S(2)}, u32[]{:S(2)}) %all-to-all-start) | async-done | bytes 65568 | tf_op jit(solution)/shard_map/all_to_all | solution.py:187
  28.0 4.4 all-to-all-start.1
  32.5 9.8 %all-to-all-done.1 = f32[1,64,2,128]{3,2,0,1:T(2,128)S(1)} async-done(((f32[1,64,2,128]{3,2,0,1:T(2,128)}), f32[1,64,2,128]{3,2,0,1:T(2,128)S(1)}, u32[]{:S(2)}, u32[]{:S(2)}) %all-to-all-start.1) | async-done | bytes 65568 | tf_op jit(solution)/shard_map/all_to_all | solution.py:194
  42.3 102.3 %scatter_custom_fusion.2 = f32[262144]{0:T(1024)S(1)} fusion(s32[16384]{0:T(1024)S(1)} %bitcast.186, f32[16384]{0:T(1024)S(1)} %bitcast.185, f32[]{:T(128)} %constant.153.clone.1), kind=kCustom, calls=%fused_computation.52 | custom fusion | flops 16384 | bytes 1048580 | tf_op jit(solution)/shard_map/scatter-add | solution.py:203
  144.6 0.3 reshape_reshape_squeeze.3
  144.9 3.5 convolution_bitcast_fusion.1
  148.4 1.0 multiply_subtract_fusion.3
  149.3 3.8 fusion.17
  153.2 0.6 copy.90
  153.8 7.5 %all_to_all.47 = f32[32,2,2,64,128]{4,0,3,2,1:T(8,128)S(1)} all-to-all(f32[32,2,2,64,128]{4,0,3,2,1:T(8,128)S(1)} %copy.90), channel_id=1, replica_groups=mesh['chan'=4,'slab_0'=4,'slab_1'=8,'slab_2'=2] {'slab_2'}, dimensions={1} | all-to-all | bytes 8388608 | tf_op jit(solution)/shard_map/all_to_all | solution.py:32
  161.3 5.2 copy.91
  166.5 4.9 all-to-all-start.3
  171.4 0.1 fusion.121
  171.6 0.1 fusion.102
  171.8 0.3 fusion.98
  172.1 0.3 fusion.87
  172.4 91.4 %all-to-all-done.3 = f32[32,2,2,64,128]{4,1,3,2,0:T(2,128)} async-done(((f32[32,2,2,64,128]{4,1,3,2,0:T(2,128)}), f32[32,2,2,64,128]{4,1,3,2,0:T(2,128)}, u32[]{:S(2)}, u32[]{:S(2)}) %all-to-all-start.3) | async-done | bytes 4194336 | tf_op jit(solution)/shard_map/all_to_all | solution.py:32
  263.9 4.6 copy.92
  268.5 7.2 %convolution_bitcast_fusion = f32[2,128,64,128]{3,1,2,0:T(8,128)S(1)} fusion(f32[2,64,64,128,1]{3,1,0,2,4:T(8,128)S(1)} %bitcast.177, f32[1,64,2,128]{3,1,2,0:T(8,128)S(1)} %get-tuple-element.21, f32[1,64,2,128]{3,1,2,0:T(8,128)S(1)} %get-tuple-element.20), kind=kOutput, calls=%fused_computation.39 | convolution fusion | flops 3221258240 | bytes 12713984 | tf_op jit(solution)/shard_map/sabc,satk->tkbc/dot_general | solution.py:93
  275.6 3.2 multiply_subtract_fusion.1
  278.8 1.1 pad_maximum_fusion
  279.9 12.5 %fusion.20 = f32[2,64,128,128]{3,1,2,0:T(8,128)S(1)} fusion(f32[2,128,64,128]{3,1,2,0:T(8,128)S(1)} %pad_maximum_fusion, f32[1,64,2,64]{1,3,0,2:T(8,128)S(1)} %get-tuple-element.23, f32[1,64,2,64]{1,3,0,2:T(8,128)S(1)} %get-tuple-element.22), kind=kOutput, calls=%fused_computation.37 | convolution fusion | flops 3221241856 | bytes 16842752 | tf_op jit(solution)/shard_map/skbc,sbtj->tjkc/dot_general | solution.py:93
  292.4 1.7 fusion.135
  294.0 2.4 copy.95
  296.5 4.4 copy.96
  300.9 8.8 %fusion.15 = (f32[1,8192,128]{2,1,0:T(8,128)}, f32[1,8192,128]{2,1,0:T(8,128)}) fusion(f32[1,8192,128]{2,1,0:T(8,128)} %param.15, f32[1,64,128,128]{3,2,1,0:T(8,128)} %copy.96, f32[1,8192,128]{2,1,0:T(8,128)} %param.14, f32[1,64,128,128]{3,2,1,0:T(8,128)S(1)} %copy.95), kind=kLoop, calls=%fused_computation.25 | loop fusion | flops 6291456 | bytes 25165824 | tf_op jit(solution)/shard_map/sub | solution.py:101
  309.7 4.8 copy.97
  314.4 2.6 copy.98
  317.1 7.7 %fusion.23 = f32[2,128,64,128]{3,1,2,0:T(8,128)S(1)} fusion(f32[1,128,64,128]{3,1,0,2:T(8,128)S(1)} %copy.98, f32[1,128,64,128]{3,1,0,2:T(8,128)S(1)} %copy.97, f32[1,128,2,128]{1,3,0,2:T(8,128)S(1)} %get-tuple-element.19, f32[1,128,2,128]{1,3,0,2:T(8,128)S(1)} %get-tuple-element.18), kind=kOutput, calls=%fused_computation.38 | convolution fusion | flops 6444613632 | bytes 17039360 | tf_op jit(solution)/shard_map/sabc,sate->tebc/dot_general | solution.py:93
  324.8 3.2 multiply_subtract_fusion
  328.0 1.1 pad_maximum_fusion.1
  329.1 9.4 %bitcast_multiply_fusion = f32[2,32,128,128]{3,1,2,0:T(8,128)S(1)} fusion(f32[2,128,64,128]{3,1,2,0:T(8,128)S(1)} %pad_maximum_fusion.1, f32[1,64,2,32]{1,3,0,2:T(8,128)S(1)} %get-tuple-element.25, f32[1,64,2,32]{1,3,0,2:T(8,128)S(1)} %get-tuple-element.24), kind=kOutput, calls=%fused_computation.22 | convolution fusion | flops 1611669504 | bytes 12615680 | tf_op jit(solution)/shard_map/sebc,sbtd->tdec/dot_general | solution.py:93
  338.6 2.4 copy.100
  341.0 15.6 %copy.101 = f32[2,4096,128]{2,0,1:T(2,128)S(1)} copy(f32[2,4096,128]{2,1,0:T(8,128)S(1)} %bitcast.180) | data formatting | bytes 8388608 | tf_op jit(solution)/shard_map/mul | solution.py:142
  356.7 106.6 %all_to_all.48 = f32[2,4096,128]{2,0,1:T(2,128)S(1)} all-to-all(f32[2,4096,128]{2,0,1:T(2,128)S(1)} %copy.101), channel_id=1, replica_groups=mesh['chan'=4,'slab_0'=4,'slab_1'=8,'slab_2'=2] {'slab_0','slab_1','slab..., dimensions={1} | all-to-all | bytes 8388608 | tf_op jit(solution)/shard_map/all_to_all | solution.py:209
  463.3 4.4 copy.152
  467.7 7.0 %reshape.554 = f32[2,64,128,64]{3,2,1,0:T(8,128)} reshape(f32[2,64,64,128]{3,2,1,0:T(8,128)} %bitcast.178) | data formatting | bytes 8388608 | tf_op jit(solution)/shard_map/reshape | solution.py:148
  474.6 15.6 %fusion.26 = f32[2,64,128,64]{2,3,1,0:T(8,128)S(1)} fusion(f32[2,64,128,64]{3,2,1,0:T(8,128)} %reshape.554, f32[1,128,2,128]{1,3,0,2:T(8,128)S(1)} %get-tuple-element.19, f32[1,128,2,128]{1,3,0,2:T(8,128)S(1)} %get-tuple-element.18), kind=kOutput, calls=%fused_computation.41 | convolution fusion | flops 3221291008 | bytes 8650752 | tf_op jit(solution)/shard_map/srab,sate->treb/dot_general | solution.py:93
  490.2 1.0 multiply_subtract_fusion.2
  491.2 2.2 fusion.36
  493.4 0.2 mul.859
  493.6 1.8 multiply_reduce_fusion
  495.4 0.7 broadcast_in_dim.15
  496.1 14.9 %all_to_all.49 = f32[64,1,1]{2,1,0:T(1,128)S(1)} all-to-all(f32[64,1,1]{2,1,0:T(1,128)S(1)} %broadcast_in_dim.15), channel_id=1, replica_groups=mesh['chan'=4,'slab_0'=4,'slab_1'=8,'slab_2'=2] {'slab_0','slab_1','slab..., dimensions={0} | all-to-all | bytes 512 | tf_op jit(solution)/shard_map/all_to_all | solution.py:44
  510.9 1.3 broadcast_in_dim.16
  512.2 4.7 all-to-all-start.6
  516.9 0.7 reduce_sum.32
  518.2 8.1 %all-to-all-done.6 = f32[64,1,1]{2,1,0:T(1,128)S(1)} async-done(((f32[64,1,1]{2,1,0:T(1,128)}), f32[64,1,1]{2,1,0:T(1,128)S(1)}, u32[]{:S(2)}, u32[]{:S(2)}) %all-to-all-start.6) | async-done | bytes 288 | tf_op jit(solution)/shard_map/all_to_all | solution.py:44
  526.3 0.7 reduce_max.19
  527.0 0.7 maximum_bitcast_fusion.15
  527.7 8.0 %all-gather = f32[4,1,2]{2,1,0:T(1,128)S(1)} all-gather(f32[1,1,2]{2,1,0:T(1,128)S(1)} %maximum_bitcast_fusion.15), channel_id=1, replica_groups=mesh['chan'=4,'slab_0'=4,'slab_1'=8,'slab_2'=2] {'chan'}, dimensions={0}, use_global_device_ids=true | all-gather | bytes 40 | tf_op jit(solution)/shard_map/all_gather | solution.py:61
  535.7 0.5 slice_bitcast_fusion
  (12 shorter events, 0.4 us)
Async XLA Ops:
  5.3 22.8 %all-to-all-start = ((s32[64,2,128]{2,1,0:T(2,128)}), s32[64,2,128]{2,1,0:T(2,128)S(1)}, u32[]{:S(2)}, u32[]{:S(2)}) async-start(s32[64,2,128]{2,1,0:T(2,128)} %bitcast.27), calls=%async_computation | async-start | bytes 131072 | tf_op jit(solution)/shard_map/all_to_all | solution.py:187
  28.0 14.3 %all-to-all-start.1 = ((f32[1,64,2,128]{3,2,0,1:T(2,128)}), f32[1,64,2,128]{3,2,0,1:T(2,128)S(1)}, u32[]{:S(2)}, u32[]{:S(2)}) async-start(f32[1,64,2,128]{3,2,0,1:T(2,128)} %bitcast.31), calls=%async_computation.1 | async-start | bytes 131072 | tf_op jit(solution)/shard_map/all_to_all | solution.py:194
  166.5 97.4 %all-to-all-start.3 = ((f32[32,2,2,64,128]{4,1,3,2,0:T(2,128)}), f32[32,2,2,64,128]{4,1,3,2,0:T(2,128)}, u32[]{:S(2)}, u32[]{:S(2)}) async-start(f32[32,2,2,64,128]{4,1,3,2,0:T(2,128)} %copy.91), calls=%async_computation.3 | async-start | bytes 8388608 | tf_op jit(solution)/shard_map/all_to_all | solution.py:32
  309.7 4.8 copy-start
  491.2 2.4 copy-start.1
  512.2 14.1 %all-to-all-start.6 = ((f32[64,1,1]{2,1,0:T(1,128)}), f32[64,1,1]{2,1,0:T(1,128)S(1)}, u32[]{:S(2)}, u32[]{:S(2)}) async-start(f32[64,1,1]{2,1,0:T(1,128)} %broadcast_in_dim.16), calls=%async_computation.6 | async-start | bytes 65536 | tf_op jit(solution)/shard_map/all_to_all | solution.py:44
where the time goes:
time: 541 us; the launch traced here: 536 us
  blocking collectives  137 us (25%)
  other arithmetic  133 us (25%)
  waiting for transfers between devices  117 us (22%)
  matrix products  61.8 us (11%)
  local copies, waits for them, and re-layouts  58.7 us (11%)
  starting transfers between devices  26.9 us (5%)
    all_to_all x1, blocking collectives, on_device(): lax.all_to_all(narrowed, SLAB, split_axis=1, concat_axis=2, tiled=True)  107 us
    scatter-add x1, other arithmetic, on_device(): jnp.zeros((chan_local, slab_area), jnp.float32).at[:, targets].add(amounts)  102 us
    all_to_all x1, waiting for transfers between devices, turned_blocks(): lax.all_to_all(pieces, axes[k], split_axis=k, concat_axis=k, tiled=True)  91.4 us
    dot_general x8, matrix products, contract(): return jnp.einsum(pattern, first_op, second_op, precision=PRECISE)  61.8 us
    mul x2, local copies, waits for them, and re-layouts, inverse_cols(): return result.reshape(2, length // 2, col_count) * (1.0 / length)  18.1 us
    sub x5, other arithmetic, twiddle(): value_re * phase_re - value_im * phase_im  17.1 us
    all_to_all x1, blocking collectives, sent_to_all(): return lax.all_to_all(copies, axis, split_axis=0, concat_axis=0, tiled=True)  14.9 us
    all_to_all x1, starting transfers between devices, on_device(): lax.all_to_all(pixel_box.reshape(slab_count, send_slots, comp_slots), SLA...  13 us
  transfers between devices with their start and end apart: 4, of which 4 were waited for; matrix products, arithmetic and copies ran while one was open for 1% of the time, Pallas kernels for 0%

commit v1 on v0

v1 whole, which is shorter than its diff:
```python
import math

import jax
import jax.numpy as jnp
import ml_dtypes
import numpy as np
from jax import lax
from jax.experimental import pallas as pl
from jax.experimental.pallas import tpu as pltpu
from jax.sharding import Mesh
from jax.sharding import PartitionSpec as P

SLAB = ("slab_0", "slab_1", "slab_2")
BF = jnp.bfloat16
F32 = jnp.float32
NT = (((1,), (1,)), ((), ()))
NN = (((1,), (0,)), ((), ()))


def halves(values):
    values = np.asarray(values, np.float32)
    high = values.astype(ml_dtypes.bfloat16)
    low = (values - high.astype(np.float32)).astype(ml_dtypes.bfloat16)
    return high, low


def phase(product, length):
    angle = 2.0 * math.pi * (np.asarray(product, np.int64) % length) / length
    return np.cos(angle), np.sin(angle)


def split(x):
    high = x.astype(BF)
    return high, (x - high.astype(F32)).astype(BF)


def mul(a, b, dims=NN):
    return lax.dot_general(a, b, dims, preferred_element_type=F32)


def dot3(a, b, dims=NN):
    return mul(a[0], b[0], dims) + (mul(a[0], b[1], dims) + mul(a[1], b[0], dims))


def swap(x):
    return pltpu.roll(x, 64, 1)


def signs():
    lane = lax.broadcasted_iota(jnp.int32, (1, 128), 1)
    return jnp.where(lane < 64, -1.0, 1.0).astype(F32)


def pack_body(owner, tile, counts, offsets, flux, box, tally):
    blocks = offsets.shape[0]
    owners = tally.shape[0]
    lane = lax.broadcasted_iota(jnp.int32, (1, 128), 1)
    box[...] = jnp.full(box.shape, -1.0, F32)

    def clear(i, c):
        tally[i] = 0
        return c

    lax.fori_loop(0, owners, clear, 0)

    def place(i, c):
        o = owner[i]
        slot = 2 * o + tally[o]
        tally[o] = tally[o] + 1
        pixels = offsets[pl.ds(i, 1), :] + tile[i] * 8192
        box[pl.ds(2 * slot, 1), :] = pixels.astype(F32)
        box[pl.ds(2 * slot + 1, 1), :] = jnp.where(lane < counts[i], flux[pl.ds(i, 1), :], 0.0)
        return c

    lax.fori_loop(0, blocks, place, 0)


def pack(owner, tile, counts, offsets, flux, owners):
    smem = pl.BlockSpec(memory_space=pltpu.SMEM)
    vmem = pl.BlockSpec(memory_space=pltpu.VMEM)
    return pl.pallas_call(
        pack_body,
        out_shape=jax.ShapeDtypeStruct((4 * owners, 128), F32),
        in_specs=[smem, smem, smem, vmem, vmem],
        out_specs=vmem,
        scratch_shapes=[pltpu.SMEM((owners,), jnp.int32)],
        name="pack",
    )(owner, tile, counts, offsets, flux)


def rows_tables():
    k = np.arange(64)
    a = np.arange(32)
    b = np.arange(128)
    c, s = phase(np.outer(k, a), 64)
    high, low = halves(np.concatenate([c, -s], 0))
    first = np.concatenate([high, high, low], 1)
    tc, ts = phase(np.outer(k, b), 8192)
    j = np.concatenate([np.arange(0, 128, 2), np.arange(1, 128, 2)])
    c, s = phase(np.outer(j, b), 128)
    wh, wl = halves(np.concatenate([c[:64], -s[:64], c[64:], -s[64:]], 0))
    return first, tc.astype(np.float32), (-ts).astype(np.float32), wh, wl


def rows_body(tiles, got, first, tc, ts, wh, wl, out0, out1, raster):
    raster[...] = jnp.zeros(raster.shape, F32)
    row_ids = lax.broadcasted_iota(jnp.int32, (64, 128), 0)
    col_ids = lax.broadcasted_iota(jnp.int32, (128, 128), 0)

    def block(i, c):
        tile = tiles[i]

        @pl.when(tile >= 0)
        def _():
            spot = got[pl.ds(2 * i, 1), :].astype(jnp.int32)
            amount = got[pl.ds(2 * i + 1, 1), :]
            high = amount.astype(BF).astype(F32)
            low = amount - high
            here = row_ids == ((spot >> 7) & 63)
            left = jnp.concatenate(
                [jnp.where(here, high, 0.0), jnp.where(here, low, 0.0)], 1
            ).astype(BF)
            there = jnp.where(col_ids == (spot & 127), 1.0, 0.0).astype(BF)
            right = jnp.concatenate([there, there], 1)
            start = pl.multiple_of(tile * 64, 64)
            raster[pl.ds(start, 64), :] = raster[pl.ds(start, 64), :] + mul(left, right, NT)

        return c

    lax.fori_loop(0, got.shape[0] // 2, block, 0)
    sg = signs()

    def row(r, c):
        xh, xl = split(raster[pl.ds(r, 32, stride=64), :])
        part = mul(first[...], jnp.concatenate([xh, xl, xh], 0))
        re, im = part[:64], part[64:]
        part = jnp.concatenate([re * tc[...] - im * ts[...], re * ts[...] + im * tc[...]], 0)
        whole = dot3((wh[...], wl[...]), split(part), NT)
        out0[pl.ds(r, 64, stride=64), :] = whole[:64] + sg * swap(whole[64:128])
        out1[pl.ds(r, 64, stride=64), :] = whole[128:192] + sg * swap(whole[192:])
        return c

    lax.fori_loop(0, 64, row, 0, unroll=2)


def forward_rows(tiles, got):
    smem = pl.BlockSpec(memory_space=pltpu.SMEM)
    vmem = pl.BlockSpec(memory_space=pltpu.VMEM)
    tables = [jnp.asarray(t) for t in rows_tables()]
    piece = jax.ShapeDtypeStruct((4096, 128), F32)
    return pl.pallas_call(
        rows_body,
        out_shape=(piece, piece),
        in_specs=[smem] + [vmem] * (1 + len(tables)),
        out_specs=(vmem, vmem),
        scratch_shapes=[pltpu.VMEM((2048, 128), F32)],
        compiler_params=pltpu.CompilerParams(vmem_limit_bytes=40 << 20),
        name="rows",
    )(tiles, got, *tables)


def cols_tables():
    k = np.arange(128)
    a = np.arange(64)
    b = np.arange(64)
    c, s = phase(np.outer(k, a), 128)
    high, low = halves(np.concatenate([c, -s], 0))
    first = np.concatenate([high, high, low], 1)
    tc, ts = phase(np.outer(k, b), 8192)
    wc, ws = phase(np.outer(b, b), 64)
    ih, il = halves(np.concatenate([wc, ws], 0))
    ec, es = phase(np.outer(a, k), 128)
    uc, us = phase(np.outer(b, k), 8192)
    f = np.float32
    return (
        first,
        tc.astype(f),
        (-ts).astype(f),
        wc.astype(f),
        (-ws).astype(f),
        ih,
        il,
        ec.astype(f),
        es.astype(f),
        uc.astype(f),
        us.astype(f),
    )


def cols_body(half, x, pr, pi, first, tc, ts, wc, ws, ih, il, ec, es, uc, us, out, mid):
    sg = signs()
    lane = lax.broadcasted_iota(jnp.int32, (1, 128), 1)
    own = (lane < 64) if half == 0 else (lane >= 64)

    def one(b, c):
        xh, xl = split(x[pl.ds(b, 64, stride=64), :])
        whole = mul(first[...], jnp.concatenate([xh, xl, xh], 0))
        mid[pl.ds(b, 128, stride=64), :] = whole[:128] + sg * swap(whole[128:])
        return c

    lax.fori_loop(0, 64, one, 0, unroll=2)

    def two(k, c):
        start = pl.multiple_of(k * 64, 64)
        value = split(mid[pl.ds(start, 64), :])
        c_row = tc[pl.ds(k, 1), :]
        s_row = ts[pl.ds(k, 1), :]
        re = wc[...] * c_row - ws[...] * s_row
        im = wc[...] * s_row + ws[...] * c_row
        whole = dot3(split(jnp.concatenate([re, im], 0)), value)
        spec = whole[:64] + sg * swap(whole[64:])
        fr = pr[pl.ds(k, 64, stride=128), :]
        fi = pi[pl.ds(k, 64, stride=128), :]
        fr = jnp.where(own, fr, swap(fr))
        fi = jnp.where(own, fi, swap(fi))
        spec = spec * fr + swap(spec) * (sg * fi)
        whole = dot3((ih[...], il[...]), split(spec))
        mid[pl.ds(start, 64), :] = whole[:64] + sg * swap(whole[64:])
        return c

    lax.fori_loop(0, 128, two, 0, unroll=2)

    def three(b, c):
        value = split(mid[pl.ds(b, 128, stride=64), :])
        c_row = uc[pl.ds(b, 1), :]
        s_row = us[pl.ds(b, 1), :]
        re = ec[...] * c_row - es[...] * s_row
        im = ec[...] * s_row + es[...] * c_row
        whole = dot3(split(jnp.concatenate([re, im], 0)), value)
        out[pl.ds(b, 64, stride=64), :] = whole[:64] + sg * swap(whole[64:])
        return c

    lax.fori_loop(0, 64, three, 0, unroll=2)


def columns(half, x, pr, pi):
    vmem = pl.BlockSpec(memory_space=pltpu.VMEM)
    tables = [jnp.asarray(t) for t in cols_tables()]
    return pl.pallas_call(
        lambda *refs: cols_body(half, *refs),
        out_shape=jax.ShapeDtypeStruct((4096, 128), F32),
        in_specs=[vmem] * (3 + len(tables)),
        out_specs=vmem,
        scratch_shapes=[pltpu.VMEM((8192, 128), F32)],
        compiler_params=pltpu.CompilerParams(vmem_limit_bytes=40 << 20),
        cost_estimate=pl.CostEstimate(flops=3 << 30, bytes_accessed=12 << 20, transcendentals=0),
        name=f"cols{half}",
    )(x, pr, pi, *tables)


def back_tables(half):
    k = np.arange(64)
    a = np.arange(32)
    b = np.arange(128)
    j = np.arange(half, 128, 2)
    c, s = phase(np.outer(b, j), 128)
    wh, wl = halves(np.concatenate([c, s], 0))
    tc, ts = phase(np.outer(b, k), 8192)
    tc = np.concatenate([tc, tc], 1).astype(np.float32)
    ts = np.concatenate([-ts, ts], 1).astype(np.float32)
    c, s = phase(np.outer(a, k), 64)
    mh, ml = halves(np.concatenate([c, -s], 1) / (8192.0 * 8192.0))
    return wh, wl, tc, ts, mh, ml


def back_body(y, base, wh, wl, tc, ts, mh, ml, out, stats, image):
    sg = signs()

    def row(r, c):
        value = split(y[pl.ds(r, 64, stride=64), :])
        whole = dot3((wh[...], wl[...]), value)
        part = whole[:128] + sg * swap(whole[128:])
        part = part * tc[...] + swap(part) * ts[...]
        image[pl.ds(r, 32, stride=64), :] = dot3((mh[...], ml[...]), split(part), NT)
        return c

    lax.fori_loop(0, 64, row, 0, unroll=2)
    total = jnp.zeros((64, 128), F32)
    top = jnp.zeros((64, 128), F32)
    for a in range(32):
        left = base[:, 128 * a : 128 * a + 128] - image[64 * a : 64 * a + 64, :]
        out[:, 128 * a : 128 * a + 128] = left
        total = total + left * left
        top = jnp.maximum(top, jnp.abs(left))
    total = jnp.sum(jnp.sum(total, axis=0, keepdims=True), axis=1, keepdims=True)
    top = jnp.max(jnp.max(top, axis=0, keepdims=True), axis=1, keepdims=True)
    where = lax.broadcasted_iota(jnp.int32, stats.shape, 1)
    stats[...] = jnp.where(where == 0, total, top)


def backward_rows(half, y, base):
    vmem = pl.BlockSpec(memory_space=pltpu.VMEM)
    tables = [jnp.asarray(t) for t in back_tables(half)]
    return pl.pallas_call(
        back_body,
        out_shape=(
            jax.ShapeDtypeStruct(base.shape, F32),
            jax.ShapeDtypeStruct((64, 128), F32),
        ),
        in_specs=[vmem] * (2 + len(tables)),
        out_specs=(vmem, vmem),
        scratch_shapes=[pltpu.VMEM((2048, 128), F32)],
        compiler_params=pltpu.CompilerParams(vmem_limit_bytes=40 << 20),
        name=f"back{half}",
    )(y, base, *tables)


def exchange(x):
    pieces = x.reshape(64, 64, 128)
    return lax.all_to_all(pieces, SLAB, split_axis=0, concat_axis=0, tiled=True).reshape(4096, 128)


def on_device(flux, offsets, counts, dest_owner, dest_tile, dirty, psf_real, psf_imag):
    slabs = lax.axis_size(SLAB)
    rows_dev, width = dirty.shape[1:]
    box = pack(dest_owner[:, 0], dest_tile, counts, offsets, flux[0], slabs)
    got = lax.all_to_all(
        box.reshape(slabs, 4, 128), SLAB, split_axis=0, concat_axis=0, tiled=True
    ).reshape(4 * slabs, 128)
    tiles = got[::2, 0].astype(jnp.int32) >> 13
    sent = forward_rows(tiles, got)
    arrived0 = exchange(sent[0])
    arrived1 = exchange(sent[1])
    back0 = exchange(columns(0, arrived0, psf_real[0], psf_imag[0]))
    back1 = exchange(columns(1, arrived1, psf_real[0], psf_imag[0]))
    partial, _ = backward_rows(0, back0, dirty[0])
    residual, stats = backward_rows(1, back1, partial)
    figures = lax.all_to_all(
        stats[:, None, :2], SLAB, split_axis=0, concat_axis=0, tiled=True
    )[:, 0]
    mean = jnp.sum(figures[:, 0]) / (rows_dev * slabs * width)
    mine = jnp.stack([jnp.sqrt(mean), jnp.max(figures[:, 1])])[None]
    every = lax.all_gather(mine, "chan", axis=0, tiled=True)
    return residual[None], every[:, 0], every[:, 1]


def solution(mesh):
    torus = Mesh(
        mesh.devices.reshape(mesh.shape["chan"], 4, 8, 2), ("chan", "slab_0", "slab_1", "slab_2")
    )
    in_specs = (
        P("chan", SLAB, None),
        P(SLAB, None),
        P(SLAB),
        P(SLAB, None),
        P(SLAB),
        P("chan", SLAB, None),
        P("chan", None, SLAB),
        P("chan", None, SLAB),
    )
    out_specs = (P("chan", SLAB, None), P(), P())
    return jax.shard_map(
        on_device, mesh=torus, in_specs=in_specs, out_specs=out_specs, check_vma=False
    )
```

time: 541 us -> 402 us (0.74)
  Pallas kernels: 0 us -> 212 us
  other arithmetic: 133 us -> 1.53 us
  waiting for transfers between devices: 117 us -> 32.8 us
  matrix products: 61.8 us -> 0 us
  local copies, waits for them, and re-layouts: 58.7 us -> 19.4 us
  blocking collectives: 137 us -> 99.6 us
  starting transfers between devices: 26.9 us -> 32.8 us
    pallas_call x0 -> x6, Pallas kernels: none -> 212 us  [the longest x2 133 us: columns(): pl.pallas_call(lambda *refs: cols_body(half, *refs), out_shape=jax.ShapeD...]
    scatter-add x1 -> x0, other arithmetic: 102 us -> none  [on_device(): jnp.zeros((chan_local, slab_area), jnp.float32).at[:, targets].add(amounts)]
    all_to_all x4, waiting for transfers between devices: 117 us -> 32.8 us  [the longest x3 24.8 us: exchange(): lax.all_to_all(pieces, SLAB, split_axis=0, concat_axis=0, tiled=True)]
    dot_general x8 -> x0, matrix products: 61.8 us -> none  [contract(): return jnp.einsum(pattern, first_op, second_op, precision=PRECISE)]
    all_to_all x3 -> x2, blocking collectives: 129 us -> 90.9 us  [the longest x1 67.6 us: exchange(): lax.all_to_all(pieces, SLAB, split_axis=0, concat_axis=0, tiled=True)]
    unnamed x4 -> x72, local copies, waits for them, and re-layouts: 0.01 us -> 18.5 us
    mul x3 -> x0, local copies, waits for them, and re-layouts: 18.3 us -> none  [the longest x2 18.1 us: inverse_cols(): return result.reshape(2, length // 2, col_count) * (1.0 / length)]
    sub x5 -> x0, other arithmetic: 17.1 us -> none  [twiddle(): value_re * phase_re - value_im * phase_im]
  transfers between devices with their start and end apart: 4 -> 4, of which waited for: 4 -> 2; matrix products, arithmetic and copies ran while one was open for 1% -> 0% of each run, Pallas kernels for 0% -> 39%
where the time goes in v1:
time: 402 us; the launch traced here: 401 us
  Pallas kernels  212 us (53%)
  blocking collectives  99.6 us (25%)
  starting transfers between devices  32.8 us (8%)
  waiting for transfers between devices  32.8 us (8%)
  local copies, waits for them, and re-layouts  19.4 us (5%)
    pallas_call x2, Pallas kernels, columns(): pl.pallas_call(lambda *refs: cols_body(half, *refs), out_shape=jax.ShapeD...  133 us
    all_to_all x1, blocking collectives, exchange(): lax.all_to_all(pieces, SLAB, split_axis=0, concat_axis=0, tiled=True)  67.6 us
    pallas_call x2, Pallas kernels, backward_rows(): pl.pallas_call(back_body, out_shape=(jax.ShapeDtypeStruct(base.shape, F32...  49.4 us
    pallas_call x1, Pallas kernels, forward_rows(): pl.pallas_call(rows_body, out_shape=(piece, piece), in_specs=[smem] + [vm...  27.7 us
    all_to_all x3, starting transfers between devices, exchange(): lax.all_to_all(pieces, SLAB, split_axis=0, concat_axis=0, tiled=True)  27 us
    all_to_all x3, waiting for transfers between devices, exchange(): lax.all_to_all(pieces, SLAB, split_axis=0, concat_axis=0, tiled=True)  24.8 us
    all_to_all x1, blocking collectives, on_device(): lax.all_to_all(box.reshape(slabs, 4, 128), SLAB, split_axis=0, concat_axi...  23.3 us
    unnamed x72, local copies, waits for them, and re-layouts  18.5 us
  transfers between devices with their start and end apart: 4, of which 2 were waited for; matrix products, arithmetic and copies ran while one was open for 0% of the time, Pallas kernels for 39%

profile of v1, /device:TPU:1, one launch (start us, length us, event | category | flops | bytes accessed | tf_op | source)
XLA Modules:
  0.0 401.0 jit_solution(15001154165769474825)
XLA Ops:
  0.6 2.4 pack.1
  3.1 23.3 %all_to_all.30 = f32[64,4,128]{2,1,0:T(4,128)S(1)} all-to-all(f32[64,4,128]{2,1,0:T(4,128)} %bitcast.37), channel_id=1, replica_groups=mesh['chan'=4,'slab_0'=4,'slab_1'=8,'slab_2'=2] {'slab_0','slab_1','slab..., dimensions={0} | all-to-all | bytes 262144 | tf_op jit(solution)/shard_map/all_to_all | solution.py:317
  26.4 0.1 shift-right-arithmetic_reduce_fusion.tiles
  26.5 0.0 copy-start.11
  26.5 0.8 copy-done.11
  27.3 0.8 copy-done.24
  28.1 0.8 copy-done.25
  28.9 0.8 copy-done.32
  29.7 0.8 copy-done.33
  30.5 27.7 %rows.1 = (f32[4096,128]{1,0:T(8,128)S(1)}, f32[4096,128]{1,0:T(8,128)S(1)}) custom-call(s32[128]{0:T(128)S(1)} %shift-right-arithmetic_reduce_fusion.tiles, f32[256,128]{1,0:T(8,128)S(1)} %bitcast.36, bf16[128,96]{1,0:T(8,128)(2,1)S(1)} %copy-done.32, f32[64,128]{1,0:T(8,128)S(1)} %copy-done.11, f32[64,128]{1,0:T(8,128)S(1)} %copy-done.33, ...), custom_call_target="tpu_custom_call" | custom-call | tf_op jit(solution)/shard_map/rows/pallas_call | solution.py:151
  58.1 0.0 copy-start.6
  58.2 67.6 %all_to_all.31 = f32[64,64,128]{2,1,0:T(8,128)} all-to-all(f32[64,64,128]{2,1,0:T(8,128)S(1)} %bitcast.33), channel_id=1, replica_groups=mesh['chan'=4,'slab_0'=4,'slab_1'=8,'slab_2'=2] {'slab_0','slab_1','slab..., dimensions={0} | all-to-all | bytes 4194304 | tf_op jit(solution)/shard_map/all_to_all | solution.py:310
  125.8 0.0 copy-done.6
  125.8 0.0 copy-start.14
  125.8 0.0 copy-start.17
  125.8 0.0 copy-start.18
  125.8 0.0 copy-start.19
  125.8 0.0 copy-start.20
  125.8 0.0 copy-start.21
  125.9 0.0 copy-start.22
  125.9 0.0 copy-start.23
  125.9 6.0 %all-to-all-start.1 = ((f32[64,64,128]{2,1,0:T(8,128)}), f32[64,64,128]{2,1,0:T(8,128)S(1)}, u32[]{:S(2)}, u32[]{:S(2)}) async-start(f32[64,64,128]{2,1,0:T(8,128)} %bitcast.32), calls=%async_computation.1 | async-start | bytes 4194304 | tf_op jit(solution)/shard_map/all_to_all | solution.py:310
  131.9 0.0 copy-done.10
  131.9 0.0 copy-done.12
  131.9 0.0 copy-done.13
  131.9 0.0 copy-done.14
  131.9 0.0 copy-done.17
  131.9 0.0 copy-done.18
  131.9 0.0 copy-done.19
  131.9 0.0 copy-done.20
  132.0 0.0 copy-start
  132.0 2.2 copy-done
  134.2 2.2 copy-done.2
  136.4 1.6 copy-done.5
  138.0 65.8 %cols0.1 = f32[4096,128]{1,0:T(8,128)S(1)} custom-call(f32[4096,128]{1,0:T(8,128)S(1)} %bitcast.30, f32[8192,128]{1,0:T(8,128)S(1)} %bitcast.24, f32[8192,128]{1,0:T(8,128)S(1)} %bitcast.26, bf16[256,192]{1,0:T(8,128)(2,1)S(1)} %copy-done.10, f32[128,64]{1,0:T(8,128)S(1)} %copy-done.13, f32[128,64]{1,0:T(8,128)S(1)} %copy-done.14, f32[64,64]{1,0:T(8,128)S(1)} %copy-done.17, ...), custom_call_target="tpu_custom_call" | custom-call | flops 3221225472 | bytes 12582912 | tf_op jit(solution)/shard_map/cols0/pallas_call | solution.py:239
  203.8 1.3 copy-done.4
  205.1 0.0 all-to-all-done.1
  205.1 10.5 %all-to-all-start.4 = ((f32[64,64,128]{2,1,0:T(8,128)}), f32[64,64,128]{2,1,0:T(8,128)}, u32[]{:S(2)}, u32[]{:S(2)}) async-start(f32[64,64,128]{2,1,0:T(8,128)} %bitcast.29), calls=%async_computation.4 | async-start | bytes 4194304 | tf_op jit(solution)/shard_map/all_to_all | solution.py:310
  215.6 0.0 copy-start.1
  215.6 2.2 copy-done.1
  217.8 2.2 copy-done.3
  220.0 67.2 %cols1.1 = f32[4096,128]{1,0:T(8,128)} custom-call(f32[4096,128]{1,0:T(8,128)S(1)} %bitcast.28, f32[8192,128]{1,0:T(8,128)S(1)} %bitcast.25, f32[8192,128]{1,0:T(8,128)S(1)} %bitcast.27, bf16[256,192]{1,0:T(8,128)(2,1)S(1)} %copy-done.10, f32[128,64]{1,0:T(8,128)S(1)} %copy-done.13, f32[128,64]{1,0:T(8,128)S(1)} %copy-done.14, f32[64,64]{1,0:T(8,128)S(1)} %copy-done.17, ...), custom_call_target="tpu_custom_call" | custom-call | flops 3221225472 | bytes 12582912 | tf_op jit(solution)/shard_map/cols1/pallas_call | solution.py:239
  287.2 0.0 all-to-all-done.4
  287.2 0.0 copy-start.28
  287.2 0.0 copy-start.29
  287.2 0.0 copy-start.30
  287.2 0.0 copy-start.31
  287.2 10.5 %all-to-all-start.2 = ((f32[64,64,128]{2,1,0:T(8,128)}), f32[64,64,128]{2,1,0:T(8,128)S(1)}, u32[]{:S(2)}, u32[]{:S(2)}) async-start(f32[64,64,128]{2,1,0:T(8,128)} %bitcast.8), calls=%async_computation.2 | async-start | bytes 4194304 | tf_op jit(solution)/shard_map/all_to_all | solution.py:310
  297.7 0.0 copy-start.26
  297.7 0.0 copy-start.27
  297.8 25.4 %back0.1 = (f32[64,4096]{1,0:T(8,128)S(1)}, f32[64,128]{1,0:T(8,128)}) custom-call(f32[4096,128]{1,0:T(8,128)} %bitcast.13.y, f32[64,4096]{1,0:T(8,128)S(1)} %bitcast.34, bf16[256,64]{1,0:T(8,128)(2,1)S(1)} %copy-done.28, bf16[256,64]{1,0:T(8,128)(2,1)S(1)} %copy-done.29, f32[128,128]{1,0:T(8,128)S(1)} %copy-done.15, f32[128,128]{1,0:T(8,128)S(1)} %copy-done.16, ...), custom_call_target="tpu_custom_call" | custom-call | tf_op jit(solution)/shard_map/back0/pallas_call | solution.py:294
  323.2 1.0 copy-done.8
  324.2 24.8 %all-to-all-done.2 = f32[64,64,128]{2,1,0:T(8,128)S(1)} async-done(((f32[64,64,128]{2,1,0:T(8,128)}), f32[64,64,128]{2,1,0:T(8,128)S(1)}, u32[]{:S(2)}, u32[]{:S(2)}) %all-to-all-start.2) | async-done | bytes 2097184 | tf_op jit(solution)/shard_map/all_to_all | solution.py:310
  348.9 1.2 copy-done.9
  350.1 24.0 %back1.1 = (f32[64,4096]{1,0:T(8,128)}, f32[64,128]{1,0:T(8,128)}) custom-call(f32[4096,128]{1,0:T(8,128)S(1)} %bitcast.31, f32[64,4096]{1,0:T(8,128)S(1)} %copy-done.9, bf16[256,64]{1,0:T(8,128)(2,1)S(1)} %copy-done.26, bf16[256,64]{1,0:T(8,128)(2,1)S(1)} %copy-done.27, f32[128,128]{1,0:T(8,128)S(1)} %copy-done.15, f32[128,128]{1,0:T(8,128)S(1)} %copy-done.16, ...), custom_call_target="tpu_custom_call" | custom-call | tf_op jit(solution)/shard_map/back1/pallas_call | solution.py:294
  374.1 5.8 %all-to-all-start.5 = ((f32[64,1,2]{2,1,0:T(1,128)}), f32[64,1,2]{2,1,0:T(1,128)S(1)}, u32[]{:S(2)}, u32[]{:S(2)}) async-start(f32[64,1,2]{2,1,0:T(1,128)} %bitcast.21), calls=%async_computation.5 | async-start | bytes 65536 | tf_op jit(solution)/shard_map/all_to_all | solution.py:328
  380.0 0.6 dynamic-slice
  381.2 8.1 %all-to-all-done.5 = f32[64,1,2]{2,1,0:T(1,128)S(1)} async-done(((f32[64,1,2]{2,1,0:T(1,128)}), f32[64,1,2]{2,1,0:T(1,128)S(1)}, u32[]{:S(2)}, u32[]{:S(2)}) %all-to-all-start.5) | async-done | bytes 544 | tf_op jit(solution)/shard_map/all_to_all | solution.py:328
  389.3 0.1 copy.54
  389.3 0.7 slice_reduce_fusion.3
  390.7 0.8 maximum_dynamic-update-slice_fusion
  391.5 8.7 %all-reduce = f32[8]{0:T(128)S(1)} all-reduce(f32[8]{0:T(128)S(1)} %maximum_dynamic-update-slice_fusion), channel_id=2, replica_groups=mesh['chan'=4,'slab_0'=4,'slab_1'=8,'slab_2'=2] {'chan'}, use_global_device_ids=true, to_apply=%add | all-reduce | flops 8 | bytes 64
  400.2 0.1 reshape.49
  400.3 0.7 slice_reduce_fusion
  (32 shorter events, 0.1 us)
Async XLA Ops:
  26.5 0.8 copy-start.11
  27.3 0.8 copy-start.24
  28.1 0.8 copy-start.25
  28.9 0.8 copy-start.32
  29.7 0.8 copy-start.33
  58.1 67.6 %copy-start.6 = (f32[4096,128]{1,0:T(8,128)}, f32[4096,128]{1,0:T(8,128)S(1)}, u32[]{:S(2)}) copy-start(f32[4096,128]{1,0:T(8,128)S(1)} %get-tuple-element.8) | copy-start | bytes 6291460
  125.8 6.1 %copy-start.10 = (bf16[256,192]{1,0:T(8,128)(2,1)S(1)}, bf16[256,192]{1,0:T(8,128)(2,1)}, u32[]{:S(2)}) copy-start(bf16[256,192]{1,0:T(8,128)(2,1)} %constant.60.clone.refs_3_) | copy-start | bytes 294916
  125.8 6.1 %copy-start.12 = (f32[64,128]{1,0:T(8,128)S(1)}, f32[64,128]{1,0:T(8,128)}, u32[]{:S(2)}) copy-start(f32[64,128]{1,0:T(8,128)} %constant.56.clone.tc.refs_12_) | copy-start | bytes 98308
  125.8 6.1 %copy-start.13 = (f32[128,64]{1,0:T(8,128)S(1)}, f32[128,64]{1,0:T(8,128)}, u32[]{:S(2)}) copy-start(f32[128,64]{1,0:T(8,128)} %constant.61.clone.refs_4_) | copy-start | bytes 98308
  125.8 6.1 %copy-start.14 = (f32[128,64]{1,0:T(8,128)S(1)}, f32[128,64]{1,0:T(8,128)}, u32[]{:S(2)}) copy-start(f32[128,64]{1,0:T(8,128)} %constant.62.clone.refs_5_) | copy-start | bytes 98308
  125.8 6.1 %copy-start.17 = (f32[64,64]{1,0:T(8,128)S(1)}, f32[64,64]{1,0:T(8,128)}, u32[]{:S(2)}) copy-start(f32[64,64]{1,0:T(8,128)} %constant.63.clone.refs_6_) | copy-start | bytes 49156
  125.8 6.1 %copy-start.18 = (f32[64,64]{1,0:T(8,128)S(1)}, f32[64,64]{1,0:T(8,128)}, u32[]{:S(2)}) copy-start(f32[64,64]{1,0:T(8,128)} %constant.64.clone.refs_7_) | copy-start | bytes 49156
  125.8 6.1 %copy-start.19 = (bf16[128,64]{1,0:T(8,128)(2,1)S(1)}, bf16[128,64]{1,0:T(8,128)(2,1)}, u32[]{:S(2)}) copy-start(bf16[128,64]{1,0:T(8,128)(2,1)} %constant.65.clone.refs_8_) | copy-start | bytes 49156
  125.8 6.1 %copy-start.20 = (bf16[128,64]{1,0:T(8,128)(2,1)S(1)}, bf16[128,64]{1,0:T(8,128)(2,1)}, u32[]{:S(2)}) copy-start(bf16[128,64]{1,0:T(8,128)(2,1)} %constant.66.clone.refs_9_) | copy-start | bytes 49156
  125.8 6.1 %copy-start.21 = (f32[64,128]{1,0:T(8,128)S(1)}, f32[64,128]{1,0:T(8,128)}, u32[]{:S(2)}) copy-start(f32[64,128]{1,0:T(8,128)} %constant.67.clone.refs_10_) | copy-start | bytes 98308
  125.9 6.1 %copy-start.22 = (f32[64,128]{1,0:T(8,128)S(1)}, f32[64,128]{1,0:T(8,128)}, u32[]{:S(2)}) copy-start(f32[64,128]{1,0:T(8,128)} %constant.68.clone.refs_11_) | copy-start | bytes 98308
  125.9 6.1 %copy-start.23 = (f32[64,128]{1,0:T(8,128)S(1)}, f32[64,128]{1,0:T(8,128)}, u32[]{:S(2)}) copy-start(f32[64,128]{1,0:T(8,128)} %constant.69.clone.refs_13_) | copy-start | bytes 98308
  125.9 79.2 %all-to-all-start.1 = ((f32[64,64,128]{2,1,0:T(8,128)}), f32[64,64,128]{2,1,0:T(8,128)S(1)}, u32[]{:S(2)}, u32[]{:S(2)}) async-start(f32[64,64,128]{2,1,0:T(8,128)} %bitcast.32), calls=%async_computation.1 | async-start | bytes 4194304 | tf_op jit(solution)/shard_map/all_to_all | solution.py:310
  132.0 2.2 copy-start
  134.2 2.2 copy-start.2
  136.4 1.6 copy-start.5
  203.8 1.3 copy-start.4
  205.1 82.1 %all-to-all-start.4 = ((f32[64,64,128]{2,1,0:T(8,128)}), f32[64,64,128]{2,1,0:T(8,128)}, u32[]{:S(2)}, u32[]{:S(2)}) async-start(f32[64,64,128]{2,1,0:T(8,128)} %bitcast.29), calls=%async_computation.4 | async-start | bytes 4194304 | tf_op jit(solution)/shard_map/all_to_all | solution.py:310
  215.6 2.2 copy-start.1
  217.8 2.2 copy-start.3
  287.2 10.6 %copy-start.7 = (f32[1,64,4096]{2,1,0:T(8,128)S(1)}, f32[1,64,4096]{2,1,0:T(8,128)}, u32[]{:S(2)}) copy-start(f32[1,64,4096]{2,1,0:T(8,128)} %param.52) | copy-start | bytes 3145732
  287.2 10.6 %copy-start.15 = (f32[128,128]{1,0:T(8,128)S(1)}, f32[128,128]{1,0:T(8,128)}, u32[]{:S(2)}) copy-start(f32[128,128]{1,0:T(8,128)} %constant.72.clone.tc) | copy-start | bytes 196612
  287.2 10.6 %copy-start.16 = (f32[128,128]{1,0:T(8,128)S(1)}, f32[128,128]{1,0:T(8,128)}, u32[]{:S(2)}) copy-start(f32[128,128]{1,0:T(8,128)} %constant.73.clone.ts) | copy-start | bytes 196612
  287.2 10.6 %copy-start.28 = (bf16[256,64]{1,0:T(8,128)(2,1)S(1)}, bf16[256,64]{1,0:T(8,128)(2,1)}, u32[]{:S(2)}) copy-start(bf16[256,64]{1,0:T(8,128)(2,1)} %constant.70.clone.wh) | copy-start | bytes 98308
  287.2 10.6 %copy-start.29 = (bf16[256,64]{1,0:T(8,128)(2,1)S(1)}, bf16[256,64]{1,0:T(8,128)(2,1)}, u32[]{:S(2)}) copy-start(bf16[256,64]{1,0:T(8,128)(2,1)} %constant.71.clone.wl) | copy-start | bytes 98308
  287.2 10.6 %copy-start.30 = (bf16[32,128]{1,0:T(8,128)(2,1)S(1)}, bf16[32,128]{1,0:T(8,128)(2,1)}, u32[]{:S(2)}) copy-start(bf16[32,128]{1,0:T(8,128)(2,1)} %constant.74.clone.mh) | copy-start | bytes 24580
  287.2 10.6 %copy-start.31 = (bf16[32,128]{1,0:T(8,128)(2,1)S(1)}, bf16[32,128]{1,0:T(8,128)(2,1)}, u32[]{:S(2)}) copy-start(bf16[32,128]{1,0:T(8,128)(2,1)} %constant.75.clone.ml) | copy-start | bytes 24580
  287.2 61.7 %all-to-all-start.2 = ((f32[64,64,128]{2,1,0:T(8,128)}), f32[64,64,128]{2,1,0:T(8,128)S(1)}, u32[]{:S(2)}, u32[]{:S(2)}) async-start(f32[64,64,128]{2,1,0:T(8,128)} %bitcast.8), calls=%async_computation.2 | async-start | bytes 4194304 | tf_op jit(solution)/shard_map/all_to_all | solution.py:310
  297.7 51.2 %copy-start.26 = (bf16[256,64]{1,0:T(8,128)(2,1)S(1)}, bf16[256,64]{1,0:T(8,128)(2,1)}, u32[]{:S(2)}) copy-start(bf16[256,64]{1,0:T(8,128)(2,1)} %constant.76.clone.wh) | copy-start | bytes 98308
  297.7 51.2 %copy-start.27 = (bf16[256,64]{1,0:T(8,128)(2,1)S(1)}, bf16[256,64]{1,0:T(8,128)(2,1)}, u32[]{:S(2)}) copy-start(bf16[256,64]{1,0:T(8,128)(2,1)} %constant.77.clone.wl) | copy-start | bytes 98308
  323.2 1.0 copy-start.8
  324.1 55.8 %copy-start.34 = (u32[256]{0:T(256)S(1)}, u32[256]{0:T(256)}, u32[]{:S(2)}) copy-start(u32[256]{0:T(256)} %constant.84) | copy-start | bytes 3076
  348.9 1.2 copy-start.9
  374.1 15.1 %all-to-all-start.5 = ((f32[64,1,2]{2,1,0:T(1,128)}), f32[64,1,2]{2,1,0:T(1,128)S(1)}, u32[]{:S(2)}, u32[]{:S(2)}) async-start(f32[64,1,2]{2,1,0:T(1,128)} %bitcast.21), calls=%async_computation.5 | async-start | bytes 65536 | tf_op jit(solution)/shard_map/all_to_all | solution.py:328

commit v2 on v1

v2 whole, which is shorter than its diff:
```python
import math

import jax
import jax.numpy as jnp
import ml_dtypes
import numpy as np
from jax import lax
from jax.experimental import pallas as pl
from jax.experimental.pallas import tpu as pltpu
from jax.sharding import Mesh
from jax.sharding import PartitionSpec as P

SLAB = ("slab_0", "slab_1", "slab_2")
BF = jnp.bfloat16
F32 = jnp.float32
NT = (((1,), (1,)), ((), ()))
NN = (((1,), (0,)), ((), ()))


def halves(values):
    values = np.asarray(values, np.float32)
    high = values.astype(ml_dtypes.bfloat16)
    low = (values - high.astype(np.float32)).astype(ml_dtypes.bfloat16)
    return high, low


def phase(product, length):
    angle = 2.0 * math.pi * (np.asarray(product, np.int64) % length) / length
    return np.cos(angle), np.sin(angle)


def split(x):
    high = x.astype(BF)
    return high, (x - high.astype(F32)).astype(BF)


def mul(a, b, dims=NN):
    return lax.dot_general(a, b, dims, preferred_element_type=F32)


def swap(x):
    return pltpu.roll(x, 64, 1)


def signs():
    lane = lax.broadcasted_iota(jnp.int32, (1, 128), 1)
    return jnp.where(lane < 64, -1.0, 1.0).astype(F32)


def pack_body(owner, tile, counts, offsets, flux, box, tally):
    blocks = offsets.shape[0]
    owners = tally.shape[0]
    lane = lax.broadcasted_iota(jnp.int32, (1, 128), 1)
    box[...] = jnp.zeros(box.shape, F32)

    def clear(i, c):
        tally[i] = 0
        return c

    lax.fori_loop(0, owners, clear, 0)

    def place(i, c):
        o = owner[i]
        slot = 2 * o + tally[o]
        tally[o] = tally[o] + 1
        pixels = offsets[pl.ds(i, 1), :] + tile[i] * 8192
        box[pl.ds(2 * slot, 1), :] = pixels.astype(F32)
        box[pl.ds(2 * slot + 1, 1), :] = jnp.where(lane < counts[i], flux[pl.ds(i, 1), :], 0.0)
        return c

    lax.fori_loop(0, blocks, place, 0)


def pack(owner, tile, counts, offsets, flux, owners):
    smem = pl.BlockSpec(memory_space=pltpu.SMEM)
    vmem = pl.BlockSpec(memory_space=pltpu.VMEM)
    return pl.pallas_call(
        pack_body,
        out_shape=jax.ShapeDtypeStruct((4 * owners, 128), F32),
        in_specs=[smem, smem, smem, vmem, vmem],
        out_specs=vmem,
        scratch_shapes=[pltpu.SMEM((owners,), jnp.int32)],
        name="pack",
    )(owner, tile, counts, offsets, flux)


def stacked(x):
    high, low = split(x)
    return jnp.concatenate([high, low, high, low], 0)


def wide(x):
    high, low = split(x)
    return jnp.concatenate([high, high, low], 1)


def beside(x):
    high, low = split(x)
    return jnp.concatenate([high, low, high], 1)


def turned(whole, count, sg):
    return whole[:count] + sg * swap(whole[count:])


def fetch(pairs, sems):
    copies = [pltpu.make_async_copy(a, b, sems.at[n]) for n, (a, b) in enumerate(pairs)]
    for copy in copies:
        copy.start()
    return copies


def table_scratch(tables):
    return [pltpu.VMEM(t.shape, t.dtype) for t in tables]


def rows_tables(half):
    k = np.arange(64)
    a = np.arange(32)
    b = np.arange(128)
    c, s = phase(np.outer(k, a), 64)
    high, low = halves(np.concatenate([c, -s], 0))
    first = np.concatenate([high, high, low, low], 1)
    tc, ts = phase(np.outer(k, b), 8192)
    phases = np.stack([tc, -ts]).astype(np.float32)
    c, s = phase(np.outer(np.arange(half, 128, 2), b), 128)
    high, low = halves(np.concatenate([c, -s], 0))
    second = np.concatenate([high, high, low], 1)
    return first, phases, second


def raster_image(tiles, got, raster):
    raster[...] = jnp.zeros(raster.shape, F32)
    row_ids = lax.broadcasted_iota(jnp.int32, (64, 128), 0)
    col_ids = lax.broadcasted_iota(jnp.int32, (128, 128), 0)

    def image(i):
        spot = got[pl.ds(2 * i, 1), :].astype(jnp.int32)
        amount = got[pl.ds(2 * i + 1, 1), :]
        high = amount.astype(BF).astype(F32)
        low = amount - high
        here = row_ids == ((spot >> 7) & 63)
        left = jnp.concatenate([jnp.where(here, high, 0.0), jnp.where(here, low, 0.0)], 1)
        there = jnp.where(col_ids == (spot & 127), 1.0, 0.0).astype(BF)
        return mul(left.astype(BF), jnp.concatenate([there, there], 1), NT)

    def blocks(n, c):
        images = [image(8 * n + u) for u in range(8)]
        for u in range(8):
            start = pl.multiple_of(tiles[8 * n + u] * 64, 64)
            raster[pl.ds(start, 64), :] = raster[pl.ds(start, 64), :] + images[u]
        return c

    lax.fori_loop(0, got.shape[0] // 16, blocks, 0)


def transform_rows(raster, first, phases, second, out):
    sg = signs()

    def rows(n, c):
        results = []
        for u in range(4):
            r = 8 * n + 2 * u
            x = [raster[pl.ds(r + v, 32, stride=64), :] for v in range(2)]
            both = mul(first[...], stacked(jnp.concatenate(x, 1)))
            parts = []
            for v in range(2):
                re = both[:64, 128 * v : 128 * v + 128]
                im = both[64:, 128 * v : 128 * v + 128]
                parts += [re * phases[0] - im * phases[1], re * phases[1] + im * phases[0]]
            whole = mul(second[...], beside(jnp.concatenate(parts, 0)), NT)
            results += [(r + v, turned(whole[:, 128 * v : 128 * v + 128], 64, sg)) for v in range(2)]
        for r, value in results:
            out[pl.ds(r, 64, stride=64), :] = value
        return c

    lax.fori_loop(0, 8, rows, 0)


def rows0_body(tiles, got, first_h, phases_h, second_h, out, raster, first, phases, second, sems):
    copies = fetch([(first_h, first), (phases_h, phases), (second_h, second)], sems)
    raster_image(tiles, got, raster)
    for copy in copies:
        copy.wait()
    transform_rows(raster, first, phases, second, out)


def rows1_body(raster, first_h, phases_h, second_h, out, first, phases, second, sems):
    for copy in fetch([(first_h, first), (phases_h, phases), (second_h, second)], sems):
        copy.wait()
    transform_rows(raster, first, phases, second, out)


def rows_call(half, body, args, specs, with_raster):
    vmem = pl.BlockSpec(memory_space=pltpu.VMEM)
    hbm = pl.BlockSpec(memory_space=pl.ANY)
    tables = [jnp.asarray(t) for t in rows_tables(half)]
    piece = jax.ShapeDtypeStruct((4096, 128), F32)
    image = jax.ShapeDtypeStruct((2048, 128), F32)
    return pl.pallas_call(
        body,
        out_shape=(piece, image) if with_raster else piece,
        in_specs=specs + [hbm] * len(tables),
        out_specs=(vmem, vmem) if with_raster else vmem,
        scratch_shapes=table_scratch(tables) + [pltpu.SemaphoreType.DMA((len(tables),))],
        compiler_params=pltpu.CompilerParams(vmem_limit_bytes=40 << 20),
        cost_estimate=pl.CostEstimate(flops=1 << 30, bytes_accessed=4 << 20, transcendentals=0),
        name=f"rows{half}",
    )(*args, *tables)


def forward_rows(tiles, got):
    smem = pl.BlockSpec(memory_space=pltpu.SMEM)
    vmem = pl.BlockSpec(memory_space=pltpu.VMEM)
    out0, raster = rows_call(0, rows0_body, (tiles, got), [smem, vmem], True)
    return out0, rows_call(1, rows1_body, (raster,), [vmem], False)


def cols_tables():
    k = np.arange(128)
    a = np.arange(64)
    b = np.arange(64)
    c, s = phase(np.outer(k, a), 128)
    high, low = halves(np.concatenate([c, -s], 0))
    first = np.concatenate([high, high, low, low], 1)
    c, s = phase(np.outer(b, b), 64)
    high, low = halves(np.concatenate([c, s], 0))
    inner = np.concatenate([high, high, low, low], 1)
    c, s = np.concatenate([c, c], 1), np.concatenate([-s, -s], 1)
    w = np.stack([c, s]).astype(np.float32)
    c, s = phase(np.outer(k, b), 8192)
    c, s = np.concatenate([c, c], 1), np.concatenate([-s, -s], 1)
    wt = np.stack([c, s]).astype(np.float32)
    e = np.stack(phase(np.outer(a, k), 128)).astype(np.float32)
    et = np.stack(phase(np.outer(b, k), 8192)).astype(np.float32)
    return first, inner, w, wt, e, et


def cols_body(half, *refs):
    x, pr_h, pi_h = refs[:3]
    hbm_tables = refs[3:9]
    out, mid, pr, pi = refs[9:13]
    first, inner, w, wt, e, et = tables = refs[13:19]
    sems = refs[19]
    copies = fetch([*zip(hbm_tables, tables), (pr_h, pr), (pi_h, pi)], sems)
    sg = signs()
    lane = lax.broadcasted_iota(jnp.int32, (1, 128), 1)
    own = (lane < 64) if half == 0 else (lane >= 64)
    for copy in copies[:6]:
        copy.wait()

    def one(n, c):
        results = []
        for u in range(2):
            b = 4 * n + 2 * u
            value = [x[pl.ds(b + v, 64, stride=64), :] for v in range(2)]
            both = mul(first[...], stacked(jnp.concatenate(value, 1)))
            for v in range(2):
                results.append((b + v, turned(both[:, 128 * v : 128 * v + 128], 128, sg)))
        for b, value in results:
            mid[pl.ds(b, 128, stride=64), :] = value
        return c

    lax.fori_loop(0, 16, one, 0)
    for copy in copies[6:]:
        copy.wait()

    def two(n, c):
        results = []
        for u in range(2):
            filtered = []
            for v in range(2):
                k = 4 * n + 2 * u + v
                value = stacked(mid[pl.ds(pl.multiple_of(k * 64, 64), 64), :])
                c_row = wt[0, pl.ds(k, 1), :]
                s_row = wt[1, pl.ds(k, 1), :]
                turn = jnp.concatenate([w[0] * c_row - w[1] * s_row, w[0] * s_row + w[1] * c_row], 0)
                spec = turned(mul(jnp.concatenate(split(turn), 1), value), 64, sg)
                fr = pr[pl.ds(k, 64, stride=128), :]
                fi = pi[pl.ds(k, 64, stride=128), :]
                fr = jnp.where(own, fr, swap(fr))
                fi = jnp.where(own, fi, swap(fi))
                filtered.append(spec * fr + swap(spec) * (sg * fi))
            both = mul(inner[...], stacked(jnp.concatenate(filtered, 1)))
            for v in range(2):
                results.append(turned(both[:, 128 * v : 128 * v + 128], 64, sg))
        start = pl.multiple_of(n * 256, 256)
        mid[pl.ds(start, 256), :] = jnp.concatenate(results, 0)
        return c

    lax.fori_loop(0, 32, two, 0)

    def three(n, c):
        results = []
        for u in range(4):
            b = 4 * n + u
            high, low = split(mid[pl.ds(b, 128, stride=64), :])
            c_row = et[0, pl.ds(b, 1), :]
            s_row = et[1, pl.ds(b, 1), :]
            turn = jnp.concatenate([e[0] * c_row - e[1] * s_row, e[0] * s_row + e[1] * c_row], 0)
            th, tl = split(turn)
            whole = mul(jnp.concatenate([th, th], 1), jnp.concatenate([high, low], 0)) + mul(tl, high)
            results.append(turned(whole, 64, sg))
        for u in range(4):
            out[pl.ds(4 * n + u, 64, stride=64), :] = results[u]
        return c

    lax.fori_loop(0, 16, three, 0)


def columns(half, x, pr, pi):
    vmem = pl.BlockSpec(memory_space=pltpu.VMEM)
    hbm = pl.BlockSpec(memory_space=pl.ANY)
    tables = [jnp.asarray(t) for t in cols_tables()]
    return pl.pallas_call(
        lambda *refs: cols_body(half, *refs),
        out_shape=jax.ShapeDtypeStruct((4096, 128), F32),
        in_specs=[vmem] + [hbm] * (2 + len(tables)),
        out_specs=vmem,
        scratch_shapes=[pltpu.VMEM((8192, 128), F32) for _ in range(3)]
        + table_scratch(tables)
        + [pltpu.SemaphoreType.DMA((2 + len(tables),))],
        compiler_params=pltpu.CompilerParams(vmem_limit_bytes=48 << 20),
        cost_estimate=pl.CostEstimate(flops=3 << 30, bytes_accessed=12 << 20, transcendentals=0),
        name=f"cols{half}",
    )(x, pr, pi, *tables)


def back_tables(half):
    k = np.arange(64)
    a = np.arange(32)
    b = np.arange(128)
    j = np.arange(half, 128, 2)
    c, s = phase(np.outer(b, j), 128)
    high, low = halves(np.concatenate([c, s], 0))
    first = np.concatenate([high, high, low, low], 1)
    tc, ts = phase(np.outer(b, k), 8192)
    phases = np.stack([np.concatenate([tc, tc], 1), np.concatenate([-ts, ts], 1)])
    c, s = phase(np.outer(a, k), 64)
    high, low = halves(np.concatenate([c, -s], 1) / (8192.0 * 8192.0))
    second = np.concatenate([high, high, low], 1)
    return first, phases.astype(np.float32), second


def back_body(y, base_h, first_h, phases_h, second_h, out, stats, image, base, first, phases, second, sems):
    copies = fetch(
        [(first_h, first), (phases_h, phases), (second_h, second), (base_h, base)], sems
    )
    for copy in copies[:3]:
        copy.wait()
    sg = signs()

    def rows(n, c):
        results = []
        for u in range(4):
            r = 8 * n + 2 * u
            value = [y[pl.ds(r + v, 64, stride=64), :] for v in range(2)]
            both = mul(first[...], stacked(jnp.concatenate(value, 1)))
            parts = []
            for v in range(2):
                part = turned(both[:, 128 * v : 128 * v + 128], 128, sg)
                parts.append(part * phases[0] + swap(part) * phases[1])
            pair = mul(second[...], beside(jnp.concatenate(parts, 0)), NT)
            results += [(r, pair[:, :128]), (r + 1, pair[:, 128:])]
        for r, value in results:
            image[pl.ds(r, 32, stride=64), :] = value
        return c

    lax.fori_loop(0, 8, rows, 0)
    copies[3].wait()
    total = jnp.zeros((64, 128), F32)
    top = jnp.zeros((64, 128), F32)
    for a in range(32):
        left = base[:, 128 * a : 128 * a + 128] - image[64 * a : 64 * a + 64, :]
        out[:, 128 * a : 128 * a + 128] = left
        total = total + left * left
        top = jnp.maximum(top, jnp.abs(left))
    total = jnp.sum(jnp.sum(total, axis=0, keepdims=True), axis=1, keepdims=True)
    top = jnp.max(jnp.max(top, axis=0, keepdims=True), axis=1, keepdims=True)
    where = lax.broadcasted_iota(jnp.int32, stats.shape, 1)
    stats[...] = jnp.where(where == 0, total, top)


def backward_rows(half, y, base):
    vmem = pl.BlockSpec(memory_space=pltpu.VMEM)
    hbm = pl.BlockSpec(memory_space=pl.ANY)
    tables = [jnp.asarray(t) for t in back_tables(half)]
    return pl.pallas_call(
        back_body,
        out_shape=(
            jax.ShapeDtypeStruct(base.shape, F32),
            jax.ShapeDtypeStruct((1, 128), F32),
        ),
        in_specs=[vmem] + [hbm] * (1 + len(tables)),
        out_specs=(vmem, vmem),
        scratch_shapes=[pltpu.VMEM((2048, 128), F32), pltpu.VMEM(base.shape, F32)]
        + table_scratch(tables)
        + [pltpu.SemaphoreType.DMA((1 + len(tables),))],
        compiler_params=pltpu.CompilerParams(vmem_limit_bytes=40 << 20),
        name=f"back{half}",
    )(y, base, *tables)


def exchange(x, name):
    with jax.named_scope(name):
        pieces = x.reshape(64, 64, 128)
        pieces = lax.all_to_all(pieces, SLAB, split_axis=0, concat_axis=0, tiled=True)
        return pieces.reshape(4096, 128)


def on_device(flux, offsets, counts, dest_owner, dest_tile, dirty, psf_real, psf_imag):
    slabs = lax.axis_size(SLAB)
    rows_dev, width = dirty.shape[1:]
    box = pack(dest_owner[:, 0], dest_tile, counts, offsets, flux[0], slabs)
    got = lax.all_to_all(
        box.reshape(slabs, 4, 128), SLAB, split_axis=0, concat_axis=0, tiled=True
    ).reshape(4 * slabs, 128)
    tiles = got[::2, 0].astype(jnp.int32) >> 13
    with jax.named_scope("image"):
        sent = forward_rows(tiles, got)
        arrived0 = exchange(sent[0], "go0")
        arrived1 = exchange(sent[1], "go1")
        back0 = exchange(columns(0, arrived0, psf_real[0], psf_imag[0]), "come0")
        back1 = exchange(columns(1, arrived1, psf_real[0], psf_imag[0]), "come1")
        partial, _ = backward_rows(0, back0, dirty[0])
        residual, stats = backward_rows(1, back1, partial)
    ranks = ("chan",) + SLAB
    copies = jnp.broadcast_to(stats[:, None, :], (lax.axis_size(ranks), 1, 128))
    figures = lax.all_to_all(copies, ranks, split_axis=0, concat_axis=0, tiled=True)
    figures = figures.reshape(-1, slabs, 128)
    rms_values = jnp.sqrt(jnp.sum(figures[:, :, 0], axis=1) / (rows_dev * slabs * width))
    peak_values = jnp.max(figures[:, :, 1], axis=1)
    return residual[None], rms_values, peak_values


def solution(mesh):
    torus = Mesh(
        mesh.devices.reshape(mesh.shape["chan"], 4, 8, 2), ("chan", "slab_0", "slab_1", "slab_2")
    )
    in_specs = (
        P("chan", SLAB, None),
        P(SLAB, None),
        P(SLAB),
        P(SLAB, None),
        P(SLAB),
        P("chan", SLAB, None),
        P("chan", None, SLAB),
        P("chan", None, SLAB),
    )
    out_specs = (P("chan", SLAB, None), P(), P())
    return jax.shard_map(
        on_device, mesh=torus, in_specs=in_specs, out_specs=out_specs, check_vma=False
    )
```

time: 402 us -> 313 us (0.78)
  Pallas kernels: 212 us -> 141 us
  blocking collectives: 99.6 us -> 44.5 us
  waiting for transfers between devices: 32.8 us -> 84.4 us
  starting transfers between devices: 32.8 us -> 25.7 us
  local copies, waits for them, and re-layouts: 19.4 us -> 14.5 us
    all_to_all x3 -> x4, waiting for transfers between devices: 24.8 us -> 84.4 us  [exchange(): lax.all_to_all(pieces, SLAB, split_axis=0, concat_axis=0, tiled=True)]
    all_to_all x1, blocking collectives: 67.6 us -> 21.2 us  [on_device(): lax.all_to_all(copies, ranks, split_axis=0, concat_axis=0, tiled=True)]
    pallas_call x2, Pallas kernels: 133 us -> 91.7 us  [columns(): pl.pallas_call(lambda *refs: cols_body(half, *refs), out_shape=jax.ShapeD...]
    pallas_call x2, Pallas kernels: 49.4 us -> 23.8 us  [backward_rows(): pl.pallas_call(back_body, out_shape=(jax.ShapeDtypeStruct(base.shape, F32...]
    unnamed x1 -> x0, blocking collectives: 8.7 us -> none
    all_to_all x1 -> x0, waiting for transfers between devices: 8.06 us -> none  [on_device(): lax.all_to_all(stats[:, None, :2], SLAB, split_axis=0, concat_axis=0, til...]
    all_to_all x1 -> x0, starting transfers between devices: 5.83 us -> none  [on_device(): lax.all_to_all(stats[:, None, :2], SLAB, split_axis=0, concat_axis=0, til...]
    pallas_call x1 -> x2, Pallas kernels: 27.7 us -> 22.8 us  [rows_call(): pl.pallas_call(body, out_shape=(piece, image) if with_raster else piece,...]
  transfers between devices with their start and end apart: 4 -> 4, of which waited for: 2 -> 4; matrix products, arithmetic and copies ran while one was open for 0% -> 0% of each run, Pallas kernels for 39% -> 36%
where the time goes in v2:
time: 313 us; the launch traced here: 312 us
  Pallas kernels  141 us (45%)
  waiting for transfers between devices  84.4 us (27%)
  blocking collectives  44.5 us (14%)
  starting transfers between devices  25.7 us (8%)
  local copies, waits for them, and re-layouts  14.5 us (5%)
    pallas_call x2, Pallas kernels, columns(): pl.pallas_call(lambda *refs: cols_body(half, *refs), out_shape=jax.ShapeD...  91.7 us
    all_to_all x4, waiting for transfers between devices, exchange(): lax.all_to_all(pieces, SLAB, split_axis=0, concat_axis=0, tiled=True)  84.4 us
    all_to_all x4, starting transfers between devices, exchange(): lax.all_to_all(pieces, SLAB, split_axis=0, concat_axis=0, tiled=True)  25.7 us
    pallas_call x2, Pallas kernels, backward_rows(): pl.pallas_call(back_body, out_shape=(jax.ShapeDtypeStruct(base.shape, F32...  23.8 us
    all_to_all x1, blocking collectives, on_device(): lax.all_to_all(box.reshape(slabs, 4, 128), SLAB, split_axis=0, concat_axi...  23.3 us
    pallas_call x2, Pallas kernels, rows_call(): pl.pallas_call(body, out_shape=(piece, image) if with_raster else piece,...  22.8 us
    all_to_all x1, blocking collectives, on_device(): lax.all_to_all(copies, ranks, split_axis=0, concat_axis=0, tiled=True)  21.2 us
    unnamed x52, local copies, waits for them, and re-layouts  14.4 us
  transfers between devices with their start and end apart: 4, of which 4 were waited for; matrix products, arithmetic and copies ran while one was open for 0% of the time, Pallas kernels for 36%

profile of v2, /device:TPU:1, one launch (start us, length us, event | category | flops | bytes accessed | tf_op | source)
XLA Modules:
  0.0 312.0 jit_solution(10695691607260794618)
XLA Ops:
  0.6 2.4 pack.1
  3.1 23.3 %all_to_all.30 = f32[64,4,128]{2,1,0:T(4,128)S(1)} all-to-all(f32[64,4,128]{2,1,0:T(4,128)} %bitcast.34), channel_id=1, replica_groups=mesh['chan'=4,'slab_0'=4,'slab_1'=8,'slab_2'=2] {'slab_0','slab_1','slab..., dimensions={0} | all-to-all | bytes 262144 | tf_op jit(solution)/shard_map/all_to_all | solution.py:415
  26.4 0.1 shift-right-arithmetic_reduce_fusion.tiles
  26.5 0.0 copy-start.21
  26.5 0.9 copy-done.21
  27.4 0.0 copy-start.22
  27.4 0.8 copy-done.22
  28.2 0.0 copy-start.24
  28.2 0.8 copy-done.24
  29.0 14.2 %rows0.1 = (f32[4096,128]{1,0:T(8,128)S(1)}, f32[2048,128]{1,0:T(8,128)S(1)}) custom-call(s32[128]{0:T(128)S(1)} %shift-right-arithmetic_reduce_fusion.tiles, f32[256,128]{1,0:T(8,128)S(1)} %bitcast.27, bf16[128,128]{1,0:T(8,128)(2,1)S(1)} %copy-done.24, f32[2,64,128]{2,1,0:T(8,128)S(1)} %copy-done.22, bf16[128,384]{1,0:T(8,128)(2,1)S(1)} %copy-done.21), custom_call_target="tpu_custom_call" | custom-call | flops 1073741824 | bytes 4194304 | tf_op jit(solution)/shard_map/image/rows0/pallas_call | solution.py:200
  43.2 0.0 copy-start.5
  43.2 1.3 copy-done.5
  44.5 0.0 copy-start.23
  44.5 0.0 copy-start.25
  44.5 5.0 %all-to-all-start.3 = ((f32[64,64,128]{2,1,0:T(8,128)}), f32[64,64,128]{2,1,0:T(8,128)S(1)}, u32[]{:S(2)}, u32[]{:S(2)}) async-start(f32[64,64,128]{2,1,0:T(8,128)} %bitcast.24), calls=%async_computation.3 | async-start | bytes 4194304 | tf_op jit(solution)/shard_map/image/go0/all_to_all | solution.py:407
  49.5 0.0 copy-done.20
  49.5 0.0 copy-done.23
  49.5 0.0 copy-done.25
  49.5 8.6 %rows1.1 = f32[4096,128]{1,0:T(8,128)S(1)} custom-call(f32[2048,128]{1,0:T(8,128)S(1)} %get-tuple-element.8.raster, bf16[128,128]{1,0:T(8,128)(2,1)S(1)} %copy-done.25, f32[2,64,128]{2,1,0:T(8,128)S(1)} %copy-done.23, bf16[128,384]{1,0:T(8,128)(2,1)S(1)} %copy-done.20), custom_call_target="tpu_custom_call" | custom-call | flops 1073741824 | bytes 4194304 | tf_op jit(solution)/shard_map/image/rows1/pallas_call | solution.py:200
  58.1 0.0 copy-start.4
  58.2 1.3 copy-done.4
  59.5 41.2 %all-to-all-done.3 = f32[64,64,128]{2,1,0:T(8,128)S(1)} async-done(((f32[64,64,128]{2,1,0:T(8,128)}), f32[64,64,128]{2,1,0:T(8,128)S(1)}, u32[]{:S(2)}, u32[]{:S(2)}) %all-to-all-start.3) | async-done | bytes 2097184 | tf_op jit(solution)/shard_map/image/go0/all_to_all | solution.py:407
  100.7 0.0 copy-start.1
  100.7 1.3 copy-done.1
  102.0 0.0 copy-start.9
  102.0 0.0 copy-start.14
  102.0 0.0 copy-start.15
  102.0 6.0 %all-to-all-start.1 = ((f32[64,64,128]{2,1,0:T(8,128)}), f32[64,64,128]{2,1,0:T(8,128)S(1)}, u32[]{:S(2)}, u32[]{:S(2)}) async-start(f32[64,64,128]{2,1,0:T(8,128)} %bitcast.23), calls=%async_computation.1 | async-start | bytes 4194304 | tf_op jit(solution)/shard_map/image/go1/all_to_all | solution.py:407
  108.0 0.0 copy-done.9
  108.0 0.0 copy-done.10
  108.1 0.0 copy-done.12
  108.1 0.0 copy-done.13
  108.1 0.0 copy-done.14
  108.1 0.0 copy-done.15
  108.1 0.0 copy-start.2
  108.1 1.6 copy-done.2
  109.7 45.8 %cols0.1 = f32[4096,128]{1,0:T(8,128)S(1)} custom-call(f32[4096,128]{1,0:T(8,128)S(1)} %bitcast.20, f32[8192,128]{1,0:T(8,128)} %bitcast.29, f32[8192,128]{1,0:T(8,128)} %bitcast.31, bf16[256,256]{1,0:T(8,128)(2,1)S(1)} %copy-done.10, bf16[128,256]{1,0:T(8,128)(2,1)S(1)} %copy-done.15, f32[2,64,128]{2,1,0:T(8,128)S(1)} %copy-done.14, ...), custom_call_target="tpu_custom_call" | custom-call | flops 3221225472 | bytes 12582912 | tf_op jit(solution)/shard_map/image/cols0/pallas_call | solution.py:315
  155.5 0.0 copy-start.3
  155.5 1.3 copy-done.3
  156.8 2.4 all-to-all-done.1
  159.2 8.1 %all-to-all-start.4 = ((f32[64,64,128]{2,1,0:T(8,128)}), f32[64,64,128]{2,1,0:T(8,128)}, u32[]{:S(2)}, u32[]{:S(2)}) async-start(f32[64,64,128]{2,1,0:T(8,128)} %bitcast.21), calls=%async_computation.4 | async-start | bytes 4194304 | tf_op jit(solution)/shard_map/image/come0/all_to_all | solution.py:407
  167.4 45.9 %cols1.1 = f32[4096,128]{1,0:T(8,128)S(1)} custom-call(f32[4096,128]{1,0:T(8,128)S(1)} %bitcast.18, f32[8192,128]{1,0:T(8,128)} %bitcast.30, f32[8192,128]{1,0:T(8,128)} %bitcast.32, bf16[256,256]{1,0:T(8,128)(2,1)S(1)} %copy-done.10, bf16[128,256]{1,0:T(8,128)(2,1)S(1)} %copy-done.15, f32[2,64,128]{2,1,0:T(8,128)S(1)} %copy-done.14, ...), custom_call_target="tpu_custom_call" | custom-call | flops 3221225472 | bytes 12582912 | tf_op jit(solution)/shard_map/image/cols1/pallas_call | solution.py:315
  213.2 0.0 copy-start
  213.2 1.4 copy-done
  214.6 3.9 %all-to-all-done.4 = f32[64,64,128]{2,1,0:T(8,128)} async-done(((f32[64,64,128]{2,1,0:T(8,128)}), f32[64,64,128]{2,1,0:T(8,128)}, u32[]{:S(2)}, u32[]{:S(2)}) %all-to-all-start.4) | async-done | bytes 2097184 | tf_op jit(solution)/shard_map/image/come0/all_to_all | solution.py:407
  218.5 6.6 %all-to-all-start.2 = ((f32[64,64,128]{2,1,0:T(8,128)}), f32[64,64,128]{2,1,0:T(8,128)S(1)}, u32[]{:S(2)}, u32[]{:S(2)}) async-start(f32[64,64,128]{2,1,0:T(8,128)} %bitcast.19), calls=%async_computation.2 | async-start | bytes 4194304 | tf_op jit(solution)/shard_map/image/come1/all_to_all | solution.py:407
  225.1 0.0 copy-start.16
  225.1 0.0 copy-done.6
  225.1 0.0 copy-done.11
  225.1 0.0 copy-done.17
  225.1 0.0 copy-start.18
  225.1 0.8 copy-done.18
  225.9 12.5 %back0.1 = (f32[64,4096]{1,0:T(8,128)S(1)}, f32[1,128]{1,0:T(1,128)}) custom-call(f32[4096,128]{1,0:T(8,128)} %bitcast.13.y, f32[64,4096]{1,0:T(8,128)S(1)} %bitcast.25, bf16[256,256]{1,0:T(8,128)(2,1)S(1)} %copy-done.17, f32[2,128,128]{2,1,0:T(8,128)S(1)} %copy-done.11, bf16[32,384]{1,0:T(8,128)(2,1)S(1)} %copy-done.18), custom_call_target="tpu_custom_call" | custom-call | tf_op jit(solution)/shard_map/image/back0/pallas_call | solution.py:388
  238.4 0.0 copy-start.7
  238.4 1.0 copy-done.7
  239.4 36.9 %all-to-all-done.2 = f32[64,64,128]{2,1,0:T(8,128)S(1)} async-done(((f32[64,64,128]{2,1,0:T(8,128)}), f32[64,64,128]{2,1,0:T(8,128)S(1)}, u32[]{:S(2)}, u32[]{:S(2)}) %all-to-all-start.2) | async-done | bytes 2097184 | tf_op jit(solution)/shard_map/image/come1/all_to_all | solution.py:407
  276.3 0.0 copy-done.16
  276.3 1.2 copy-done.8
  277.5 0.7 copy-done.19
  278.3 11.2 %back1.1 = (f32[64,4096]{1,0:T(8,128)}, f32[1,128]{1,0:T(1,128)S(1)}) custom-call(f32[4096,128]{1,0:T(8,128)S(1)} %bitcast.22, f32[64,4096]{1,0:T(8,128)S(1)} %copy-done.8, bf16[256,256]{1,0:T(8,128)(2,1)S(1)} %copy-done.16, f32[2,128,128]{2,1,0:T(8,128)S(1)} %copy-done.11, bf16[32,384]{1,0:T(8,128)(2,1)S(1)} %copy-done.19), custom_call_target="tpu_custom_call" | custom-call | tf_op jit(solution)/shard_map/image/back1/pallas_call | solution.py:388
  289.5 0.1 broadcast_in_dim.13
  289.6 21.2 %all_to_all.31 = f32[256,1,128]{2,1,0:T(1,128)S(1)} all-to-all(f32[256,1,128]{2,1,0:T(1,128)S(1)} %broadcast_in_dim.13), channel_id=1, replica_groups=mesh['chan'=4,'slab_0'=4,'slab_1'=8,'slab_2'=2] {'chan','slab_0','slab_1..., dimensions={0} | all-to-all | bytes 262144 | tf_op jit(solution)/shard_map/all_to_all | solution.py:429
  310.8 0.7 slice_reduce_fusion
  311.5 0.5 multiply_sqrt_fusion
  (10 shorter events, 0.0 us)
Async XLA Ops:
  26.5 0.9 copy-start.21
  27.4 0.8 copy-start.22
  28.2 0.8 copy-start.24
  43.2 1.3 copy-start.5
  44.5 5.0 %copy-start.20 = (bf16[128,384]{1,0:T(8,128)(2,1)S(1)}, bf16[128,384]{1,0:T(8,128)(2,1)}, u32[]{:S(2)}) copy-start(bf16[128,384]{1,0:T(8,128)(2,1)} %constant.40.clone.second_h) | copy-start | bytes 294916
  44.5 5.0 %copy-start.23 = (f32[2,64,128]{2,1,0:T(8,128)S(1)}, f32[2,64,128]{2,1,0:T(8,128)}, u32[]{:S(2)}) copy-start(f32[2,64,128]{2,1,0:T(8,128)} %constant.38.clone.phases_h) | copy-start | bytes 196612
  44.5 5.0 %copy-start.25 = (bf16[128,128]{1,0:T(8,128)(2,1)S(1)}, bf16[128,128]{1,0:T(8,128)(2,1)}, u32[]{:S(2)}) copy-start(bf16[128,128]{1,0:T(8,128)(2,1)} %constant.37.clone.first_h) | copy-start | bytes 98308
  44.5 56.2 %all-to-all-start.3 = ((f32[64,64,128]{2,1,0:T(8,128)}), f32[64,64,128]{2,1,0:T(8,128)S(1)}, u32[]{:S(2)}, u32[]{:S(2)}) async-start(f32[64,64,128]{2,1,0:T(8,128)} %bitcast.24), calls=%async_computation.3 | async-start | bytes 4194304 | tf_op jit(solution)/shard_map/image/go0/all_to_all | solution.py:407
  58.1 1.3 copy-start.4
  100.7 1.3 copy-start.1
  102.0 6.0 %copy-start.9 = (f32[2,128,128]{2,1,0:T(8,128)S(1)}, f32[2,128,128]{2,1,0:T(8,128)}, u32[]{:S(2)}) copy-start(f32[2,128,128]{2,1,0:T(8,128)} %constant.44.clone.refs_6_) | copy-start | bytes 393220
  102.0 6.0 %copy-start.10 = (bf16[256,256]{1,0:T(8,128)(2,1)S(1)}, bf16[256,256]{1,0:T(8,128)(2,1)}, u32[]{:S(2)}) copy-start(bf16[256,256]{1,0:T(8,128)(2,1)} %constant.41.clone.refs_3_) | copy-start | bytes 393220
  102.0 6.0 %copy-start.12 = (f32[2,64,128]{2,1,0:T(8,128)S(1)}, f32[2,64,128]{2,1,0:T(8,128)}, u32[]{:S(2)}) copy-start(f32[2,64,128]{2,1,0:T(8,128)} %constant.46.clone.refs_8_) | copy-start | bytes 196612
  102.0 6.0 %copy-start.13 = (f32[2,64,128]{2,1,0:T(8,128)S(1)}, f32[2,64,128]{2,1,0:T(8,128)}, u32[]{:S(2)}) copy-start(f32[2,64,128]{2,1,0:T(8,128)} %constant.45.clone.refs_7_) | copy-start | bytes 196612
  102.0 6.0 %copy-start.14 = (f32[2,64,128]{2,1,0:T(8,128)S(1)}, f32[2,64,128]{2,1,0:T(8,128)}, u32[]{:S(2)}) copy-start(f32[2,64,128]{2,1,0:T(8,128)} %constant.43.clone.refs_5_) | copy-start | bytes 196612
  102.0 6.0 %copy-start.15 = (bf16[128,256]{1,0:T(8,128)(2,1)S(1)}, bf16[128,256]{1,0:T(8,128)(2,1)}, u32[]{:S(2)}) copy-start(bf16[128,256]{1,0:T(8,128)(2,1)} %constant.42.clone.refs_4_) | copy-start | bytes 196612
  102.0 57.2 %all-to-all-start.1 = ((f32[64,64,128]{2,1,0:T(8,128)}), f32[64,64,128]{2,1,0:T(8,128)S(1)}, u32[]{:S(2)}, u32[]{:S(2)}) async-start(f32[64,64,128]{2,1,0:T(8,128)} %bitcast.23), calls=%async_computation.1 | async-start | bytes 4194304 | tf_op jit(solution)/shard_map/image/go1/all_to_all | solution.py:407
  108.1 1.6 copy-start.2
  155.5 1.3 copy-start.3
  159.2 59.2 %all-to-all-start.4 = ((f32[64,64,128]{2,1,0:T(8,128)}), f32[64,64,128]{2,1,0:T(8,128)}, u32[]{:S(2)}, u32[]{:S(2)}) async-start(f32[64,64,128]{2,1,0:T(8,128)} %bitcast.21), calls=%async_computation.4 | async-start | bytes 4194304 | tf_op jit(solution)/shard_map/image/come0/all_to_all | solution.py:407
  213.2 1.4 copy-start
  218.5 6.6 %copy-start.6 = (f32[1,64,4096]{2,1,0:T(8,128)S(1)}, f32[1,64,4096]{2,1,0:T(8,128)}, u32[]{:S(2)}) copy-start(f32[1,64,4096]{2,1,0:T(8,128)} %param.37) | copy-start | bytes 3145732
  218.5 6.6 %copy-start.11 = (f32[2,128,128]{2,1,0:T(8,128)S(1)}, f32[2,128,128]{2,1,0:T(8,128)}, u32[]{:S(2)}) copy-start(f32[2,128,128]{2,1,0:T(8,128)} %constant.48.clone.phases_h) | copy-start | bytes 393220
  218.5 6.6 %copy-start.17 = (bf16[256,256]{1,0:T(8,128)(2,1)S(1)}, bf16[256,256]{1,0:T(8,128)(2,1)}, u32[]{:S(2)}) copy-start(bf16[256,256]{1,0:T(8,128)(2,1)} %constant.47.clone.first_h) | copy-start | bytes 393220
  218.5 57.8 %all-to-all-start.2 = ((f32[64,64,128]{2,1,0:T(8,128)}), f32[64,64,128]{2,1,0:T(8,128)S(1)}, u32[]{:S(2)}, u32[]{:S(2)}) async-start(f32[64,64,128]{2,1,0:T(8,128)} %bitcast.19), calls=%async_computation.2 | async-start | bytes 4194304 | tf_op jit(solution)/shard_map/image/come1/all_to_all | solution.py:407
  225.1 51.2 %copy-start.16 = (bf16[256,256]{1,0:T(8,128)(2,1)S(1)}, bf16[256,256]{1,0:T(8,128)(2,1)}, u32[]{:S(2)}) copy-start(bf16[256,256]{1,0:T(8,128)(2,1)} %constant.50.clone.first_h) | copy-start | bytes 393220
  225.1 0.8 copy-start.18
  238.4 1.0 copy-start.7
  276.3 1.2 copy-start.8
  277.5 0.7 copy-start.19

commit v3 on v2

--- a/solution.py
+++ b/solution.py
@@ -13,6 +13,7 @@
 SLAB = ("slab_0", "slab_1", "slab_2")
 BF = jnp.bfloat16
 F32 = jnp.float32
+GRANT = 65280 << 10
 NT = (((1,), (1,)), ((), ()))
 NN = (((1,), (0,)), ((), ()))
 
@@ -147,63 +148,80 @@
     def blocks(n, c):
         images = [image(8 * n + u) for u in range(8)]
         for u in range(8):
-            start = pl.multiple_of(tiles[8 * n + u] * 64, 64)
-            raster[pl.ds(start, 64), :] = raster[pl.ds(start, 64), :] + images[u]
+            tile = tiles[8 * n + u]
+            raster[tile] = raster[tile] + images[u]
         return c
 
     lax.fori_loop(0, got.shape[0] // 16, blocks, 0)
 
 
-def transform_rows(raster, first, phases, second, out):
+def band(source, target, sems, n):
+    rows = pl.ds(pl.multiple_of(8 * n, 8), 8)
+    return pltpu.make_async_copy(source.at[:, rows, :], target.at[:, rows, :], sems.at[n])
+
+
+def transform_rows(raster, first, phases, second, out, out_h, sems):
     sg = signs()
 
     def rows(n, c):
         results = []
+        start = pl.multiple_of(8 * n, 8)
+        lines = jnp.swapaxes(raster[:, pl.ds(start, 8), :], 0, 1)
         for u in range(4):
-            r = 8 * n + 2 * u
-            x = [raster[pl.ds(r + v, 32, stride=64), :] for v in range(2)]
-            both = mul(first[...], stacked(jnp.concatenate(x, 1)))
+            both = mul(first[...], stacked(jnp.concatenate([lines[2 * u], lines[2 * u + 1]], 1)))
             parts = []
             for v in range(2):
                 re = both[:64, 128 * v : 128 * v + 128]
                 im = both[64:, 128 * v : 128 * v + 128]
                 parts += [re * phases[0] - im * phases[1], re * phases[1] + im * phases[0]]
             whole = mul(second[...], beside(jnp.concatenate(parts, 0)), NT)
-            results += [(r + v, turned(whole[:, 128 * v : 128 * v + 128], 64, sg)) for v in range(2)]
-        for r, value in results:
-            out[pl.ds(r, 64, stride=64), :] = value
+            results += [turned(whole[:, 128 * v : 128 * v + 128], 64, sg) for v in range(2)]
+        out[:, pl.ds(start, 8), :] = jnp.swapaxes(jnp.stack(results), 0, 1)
+        band(out, out_h, sems, n).start()
         return c
 
     lax.fori_loop(0, 8, rows, 0)
-
-
-def rows0_body(tiles, got, first_h, phases_h, second_h, out, raster, first, phases, second, sems):
+    for n in range(8):
+        band(out, out_h, sems, n).wait()
+
+
+def rows0_body(
+    tiles, got, first_h, phases_h, second_h, out_h, raster_h, first, phases, second, out, raster, sems, bands
+):
     copies = fetch([(first_h, first), (phases_h, phases), (second_h, second)], sems)
     raster_image(tiles, got, raster)
+    save = pltpu.make_async_copy(raster, raster_h, sems.at[3])
+    save.start()
     for copy in copies:
         copy.wait()
-    transform_rows(raster, first, phases, second, out)
-
-
-def rows1_body(raster, first_h, phases_h, second_h, out, first, phases, second, sems):
-    for copy in fetch([(first_h, first), (phases_h, phases), (second_h, second)], sems):
+    transform_rows(raster, first, phases, second, out, out_h, bands)
+    save.wait()
+
+
+def rows1_body(
+    raster_h, first_h, phases_h, second_h, out_h, first, phases, second, out, raster, sems, bands
+):
+    for copy in fetch(
+        [(first_h, first), (phases_h, phases), (second_h, second), (raster_h, raster)], sems
+    ):
         copy.wait()
-    transform_rows(raster, first, phases, second, out)
+    transform_rows(raster, first, phases, second, out, out_h, bands)
 
 
 def rows_call(half, body, args, specs, with_raster):
-    vmem = pl.BlockSpec(memory_space=pltpu.VMEM)
-    hbm = pl.BlockSpec(memory_space=pl.ANY)
+    hbm = pl.BlockSpec(memory_space=pltpu.HBM)
     tables = [jnp.asarray(t) for t in rows_tables(half)]
-    piece = jax.ShapeDtypeStruct((4096, 128), F32)
-    image = jax.ShapeDtypeStruct((2048, 128), F32)
+    piece = jax.ShapeDtypeStruct((64, 64, 128), F32)
+    image = jax.ShapeDtypeStruct((32, 64, 128), F32)
     return pl.pallas_call(
         body,
         out_shape=(piece, image) if with_raster else piece,
         in_specs=specs + [hbm] * len(tables),
-        out_specs=(vmem, vmem) if with_raster else vmem,
-        scratch_shapes=table_scratch(tables) + [pltpu.SemaphoreType.DMA((len(tables),))],
-        compiler_params=pltpu.CompilerParams(vmem_limit_bytes=40 << 20),
+        out_specs=(hbm, hbm) if with_raster else hbm,
+        scratch_shapes=table_scratch(tables)
+        + [pltpu.VMEM(piece.shape, F32), pltpu.VMEM(image.shape, F32)]
+        + [pltpu.SemaphoreType.DMA((4,)), pltpu.SemaphoreType.DMA((8,))],
+        compiler_params=pltpu.CompilerParams(vmem_limit_bytes=GRANT),
         cost_estimate=pl.CostEstimate(flops=1 << 30, bytes_accessed=4 << 20, transcendentals=0),
         name=f"rows{half}",
     )(*args, *tables)
@@ -212,8 +230,9 @@
 def forward_rows(tiles, got):
     smem = pl.BlockSpec(memory_space=pltpu.SMEM)
     vmem = pl.BlockSpec(memory_space=pltpu.VMEM)
+    hbm = pl.BlockSpec(memory_space=pltpu.HBM)
     out0, raster = rows_call(0, rows0_body, (tiles, got), [smem, vmem], True)
-    return out0, rows_call(1, rows1_body, (raster,), [vmem], False)
+    return out0, rows_call(1, rows1_body, (raster,), [hbm], False)
 
 
 def cols_tables():
@@ -239,9 +258,9 @@
 def cols_body(half, *refs):
     x, pr_h, pi_h = refs[:3]
     hbm_tables = refs[3:9]
-    out, mid, pr, pi = refs[9:13]
-    first, inner, w, wt, e, et = tables = refs[13:19]
-    sems = refs[19]
+    out, mid, back, pr, pi = refs[9:14]
+    first, inner, w, wt, e, et = tables = refs[14:20]
+    sems = refs[20]
     copies = fetch([*zip(hbm_tables, tables), (pr_h, pr), (pi_h, pi)], sems)
     sg = signs()
     lane = lax.broadcasted_iota(jnp.int32, (1, 128), 1)
@@ -250,77 +269,76 @@
         copy.wait()
 
     def one(n, c):
-        results = []
-        for u in range(2):
-            b = 4 * n + 2 * u
-            value = [x[pl.ds(b + v, 64, stride=64), :] for v in range(2)]
-            both = mul(first[...], stacked(jnp.concatenate(value, 1)))
+        start = pl.multiple_of(8 * n, 8)
+        lines = jnp.swapaxes(x[:, pl.ds(start, 8), :], 0, 1)
+        for u in range(4):
+            both = mul(first[...], stacked(jnp.concatenate([lines[2 * u], lines[2 * u + 1]], 1)))
             for v in range(2):
-                results.append((b + v, turned(both[:, 128 * v : 128 * v + 128], 128, sg)))
-        for b, value in results:
-            mid[pl.ds(b, 128, stride=64), :] = value
-        return c
-
-    lax.fori_loop(0, 16, one, 0)
+                mid[8 * n + 2 * u + v] = turned(both[:, 128 * v : 128 * v + 128], 128, sg)
+        return c
+
+    lax.fori_loop(0, 8, one, 0)
     for copy in copies[6:]:
         copy.wait()
 
     def two(n, c):
-        results = []
-        for u in range(2):
+        start = pl.multiple_of(8 * n, 8)
+        lines = jnp.swapaxes(mid[:, pl.ds(start, 8), :], 0, 1)
+        frs = jnp.swapaxes(pr[:, pl.ds(start, 8), :], 0, 1)
+        fis = jnp.swapaxes(pi[:, pl.ds(start, 8), :], 0, 1)
+        for u in range(4):
             filtered = []
             for v in range(2):
-                k = 4 * n + 2 * u + v
-                value = stacked(mid[pl.ds(pl.multiple_of(k * 64, 64), 64), :])
+                k = 8 * n + 2 * u + v
                 c_row = wt[0, pl.ds(k, 1), :]
                 s_row = wt[1, pl.ds(k, 1), :]
                 turn = jnp.concatenate([w[0] * c_row - w[1] * s_row, w[0] * s_row + w[1] * c_row], 0)
+                value = stacked(lines[2 * u + v])
                 spec = turned(mul(jnp.concatenate(split(turn), 1), value), 64, sg)
-                fr = pr[pl.ds(k, 64, stride=128), :]
-                fi = pi[pl.ds(k, 64, stride=128), :]
+                fr = frs[2 * u + v]
+                fi = fis[2 * u + v]
                 fr = jnp.where(own, fr, swap(fr))
                 fi = jnp.where(own, fi, swap(fi))
                 filtered.append(spec * fr + swap(spec) * (sg * fi))
             both = mul(inner[...], stacked(jnp.concatenate(filtered, 1)))
             for v in range(2):
-                results.append(turned(both[:, 128 * v : 128 * v + 128], 64, sg))
-        start = pl.multiple_of(n * 256, 256)
-        mid[pl.ds(start, 256), :] = jnp.concatenate(results, 0)
-        return c
-
-    lax.fori_loop(0, 32, two, 0)
+                back[8 * n + 2 * u + v] = turned(both[:, 128 * v : 128 * v + 128], 64, sg)
+        return c
+
+    lax.fori_loop(0, 16, two, 0)
 
     def three(n, c):
+        start = pl.multiple_of(8 * n, 8)
+        lines = jnp.swapaxes(back[:, pl.ds(start, 8), :], 0, 1)
         results = []
-        for u in range(4):
-            b = 4 * n + u
-            high, low = split(mid[pl.ds(b, 128, stride=64), :])
-            c_row = et[0, pl.ds(b, 1), :]
-            s_row = et[1, pl.ds(b, 1), :]
+        for u in range(8):
+            high, low = split(lines[u])
+            c_row = et[0, pl.ds(8 * n + u, 1), :]
+            s_row = et[1, pl.ds(8 * n + u, 1), :]
             turn = jnp.concatenate([e[0] * c_row - e[1] * s_row, e[0] * s_row + e[1] * c_row], 0)
             th, tl = split(turn)
             whole = mul(jnp.concatenate([th, th], 1), jnp.concatenate([high, low], 0)) + mul(tl, high)
             results.append(turned(whole, 64, sg))
-        for u in range(4):
-            out[pl.ds(4 * n + u, 64, stride=64), :] = results[u]
-        return c
-
-    lax.fori_loop(0, 16, three, 0)
+        out[:, pl.ds(start, 8), :] = jnp.swapaxes(jnp.stack(results), 0, 1)
+        return c
+
+    lax.fori_loop(0, 8, three, 0)
 
 
 def columns(half, x, pr, pi):
     vmem = pl.BlockSpec(memory_space=pltpu.VMEM)
-    hbm = pl.BlockSpec(memory_space=pl.ANY)
+    hbm = pl.BlockSpec(memory_space=pltpu.HBM)
     tables = [jnp.asarray(t) for t in cols_tables()]
     return pl.pallas_call(
         lambda *refs: cols_body(half, *refs),
-        out_shape=jax.ShapeDtypeStruct((4096, 128), F32),
+        out_shape=jax.ShapeDtypeStruct((64, 64, 128), F32),
         in_specs=[vmem] + [hbm] * (2 + len(tables)),
         out_specs=vmem,
-        scratch_shapes=[pltpu.VMEM((8192, 128), F32) for _ in range(3)]
+        scratch_shapes=[pltpu.VMEM((64, 128, 128), F32), pltpu.VMEM((128, 64, 128), F32)]
+        + [pltpu.VMEM((64, 128, 128), F32) for _ in range(2)]
         + table_scratch(tables)
         + [pltpu.SemaphoreType.DMA((2 + len(tables),))],
-        compiler_params=pltpu.CompilerParams(vmem_limit_bytes=48 << 20),
+        compiler_params=pltpu.CompilerParams(vmem_limit_bytes=GRANT),
         cost_estimate=pl.CostEstimate(flops=3 << 30, bytes_accessed=12 << 20, transcendentals=0),
         name=f"cols{half}",
     )(x, pr, pi, *tables)
@@ -342,48 +360,59 @@
     return first, phases.astype(np.float32), second
 
 
-def back_body(y, base_h, first_h, phases_h, second_h, out, stats, image, base, first, phases, second, sems):
-    copies = fetch(
-        [(first_h, first), (phases_h, phases), (second_h, second), (base_h, base)], sems
-    )
-    for copy in copies[:3]:
+def back_body(
+    y_h, base_h, first_h, phases_h, second_h, out_h, stats, image, base, first, phases, second, y, sems, bands, ends
+):
+    copies = fetch([(first_h, first), (phases_h, phases), (second_h, second)], sems)
+    for n in range(8):
+        band(y_h, y, bands, n).start()
+    keep = pltpu.make_async_copy(base_h, base, sems.at[3])
+    keep.start()
+    for copy in copies:
         copy.wait()
     sg = signs()
 
     def rows(n, c):
         results = []
+        band(y_h, y, bands, n).wait()
+        start = pl.multiple_of(8 * n, 8)
+        lines = jnp.swapaxes(y[:, pl.ds(start, 8), :], 0, 1)
         for u in range(4):
-            r = 8 * n + 2 * u
-            value = [y[pl.ds(r + v, 64, stride=64), :] for v in range(2)]
-            both = mul(first[...], stacked(jnp.concatenate(value, 1)))
+            both = mul(first[...], stacked(jnp.concatenate([lines[2 * u], lines[2 * u + 1]], 1)))
             parts = []
             for v in range(2):
                 part = turned(both[:, 128 * v : 128 * v + 128], 128, sg)
                 parts.append(part * phases[0] + swap(part) * phases[1])
             pair = mul(second[...], beside(jnp.concatenate(parts, 0)), NT)
-            results += [(r, pair[:, :128]), (r + 1, pair[:, 128:])]
-        for r, value in results:
-            image[pl.ds(r, 32, stride=64), :] = value
+            results += [pair[:, :128], pair[:, 128:]]
+        image[:, pl.ds(start, 8), :] = jnp.swapaxes(jnp.stack(results), 0, 1)
         return c
 
     lax.fori_loop(0, 8, rows, 0)
-    copies[3].wait()
+    keep.wait()
     total = jnp.zeros((64, 128), F32)
     top = jnp.zeros((64, 128), F32)
-    for a in range(32):
-        left = base[:, 128 * a : 128 * a + 128] - image[64 * a : 64 * a + 64, :]
-        out[:, 128 * a : 128 * a + 128] = left
-        total = total + left * left
-        top = jnp.maximum(top, jnp.abs(left))
+    saves = []
+    for g in range(4):
+        for a in range(8 * g, 8 * g + 8):
+            left = base[:, 128 * a : 128 * a + 128] - image[a]
+            base[:, 128 * a : 128 * a + 128] = left
+            total = total + left * left
+            top = jnp.maximum(top, jnp.abs(left))
+        part = pl.ds(1024 * g, 1024)
+        saves.append(pltpu.make_async_copy(base.at[:, part], out_h.at[:, part], ends.at[g]))
+        saves[-1].start()
     total = jnp.sum(jnp.sum(total, axis=0, keepdims=True), axis=1, keepdims=True)
     top = jnp.max(jnp.max(top, axis=0, keepdims=True), axis=1, keepdims=True)
     where = lax.broadcasted_iota(jnp.int32, stats.shape, 1)
     stats[...] = jnp.where(where == 0, total, top)
+    for save in saves:
+        save.wait()
 
 
 def backward_rows(half, y, base):
     vmem = pl.BlockSpec(memory_space=pltpu.VMEM)
-    hbm = pl.BlockSpec(memory_space=pl.ANY)
+    hbm = pl.BlockSpec(memory_space=pltpu.HBM)
     tables = [jnp.asarray(t) for t in back_tables(half)]
     return pl.pallas_call(
         back_body,
@@ -391,21 +420,20 @@
             jax.ShapeDtypeStruct(base.shape, F32),
             jax.ShapeDtypeStruct((1, 128), F32),
         ),
-        in_specs=[vmem] + [hbm] * (1 + len(tables)),
-        out_specs=(vmem, vmem),
-        scratch_shapes=[pltpu.VMEM((2048, 128), F32), pltpu.VMEM(base.shape, F32)]
+        in_specs=[hbm] * (2 + len(tables)),
+        out_specs=(hbm, vmem),
+        scratch_shapes=[pltpu.VMEM((32, 64, 128), F32), pltpu.VMEM(base.shape, F32)]
         + table_scratch(tables)
-        + [pltpu.SemaphoreType.DMA((1 + len(tables),))],
-        compiler_params=pltpu.CompilerParams(vmem_limit_bytes=40 << 20),
+        + [pltpu.VMEM(y.shape, F32)]
+        + [pltpu.SemaphoreType.DMA((n,)) for n in (4, 8, 4)],
+        compiler_params=pltpu.CompilerParams(vmem_limit_bytes=GRANT),
         name=f"back{half}",
     )(y, base, *tables)
 
 
 def exchange(x, name):
     with jax.named_scope(name):
-        pieces = x.reshape(64, 64, 128)
-        pieces = lax.all_to_all(pieces, SLAB, split_axis=0, concat_axis=0, tiled=True)
-        return pieces.reshape(4096, 128)
+        return lax.all_to_all(x, SLAB, split_axis=0, concat_axis=0, tiled=True)
 
 
 def on_device(flux, offsets, counts, dest_owner, dest_tile, dirty, psf_real, psf_imag):
@@ -418,10 +446,11 @@
     tiles = got[::2, 0].astype(jnp.int32) >> 13
     with jax.named_scope("image"):
         sent = forward_rows(tiles, got)
+        psf = [part.reshape(64, 128, 128) for part in (psf_real, psf_imag)]
         arrived0 = exchange(sent[0], "go0")
         arrived1 = exchange(sent[1], "go1")
-        back0 = exchange(columns(0, arrived0, psf_real[0], psf_imag[0]), "come0")
-        back1 = exchange(columns(1, arrived1, psf_real[0], psf_imag[0]), "come1")
+        back0 = exchange(columns(0, arrived0, *psf), "come0")
+        back1 = exchange(columns(1, arrived1, *psf), "come1")
         partial, _ = backward_rows(0, back0, dirty[0])
         residual, stats = backward_rows(1, back1, partial)
     ranks = ("chan",) + SLAB

time: 313 us -> 305 us (0.974)
  waiting for transfers between devices: 84.4 us -> 104 us
  local copies, waits for them, and re-layouts: 14.5 us -> 0.75 us
  Pallas kernels: 141 us -> 129 us
    all_to_all x4, waiting for transfers between devices: 84.4 us -> 104 us  [exchange(): return lax.all_to_all(x, SLAB, split_axis=0, concat_axis=0, tiled=True)]
    unnamed x52 -> x2, local copies, waits for them, and re-layouts: 14.4 us -> 0.01 us
    pallas_call x2, Pallas kernels: 91.7 us -> 78.6 us  [columns(): pl.pallas_call(lambda *refs: cols_body(half, *refs), out_shape=jax.ShapeD...]
  transfers between devices with their start and end apart: 4 -> 4, of which waited for: 4 -> 4; matrix products, arithmetic and copies ran while one was open for 0% -> 0% of each run, Pallas kernels for 36% -> 33%
where the time goes in v3:
time: 305 us; the launch traced here: 304 us
  Pallas kernels  129 us (42%)
  waiting for transfers between devices  104 us (34%)
  blocking collectives  44.5 us (15%)
  starting transfers between devices  23.4 us (8%)
    all_to_all x4, waiting for transfers between devices, exchange(): return lax.all_to_all(x, SLAB, split_axis=0, concat_axis=0, tiled=True)  104 us
    pallas_call x2, Pallas kernels, columns(): pl.pallas_call(lambda *refs: cols_body(half, *refs), out_shape=jax.ShapeD...  78.6 us
    pallas_call x2, Pallas kernels, backward_rows(): pl.pallas_call(back_body, out_shape=(jax.ShapeDtypeStruct(base.shape, F32...  24.4 us
    pallas_call x2, Pallas kernels, rows_call(): pl.pallas_call(body, out_shape=(piece, image) if with_raster else piece,...  23.4 us
    all_to_all x4, starting transfers between devices, exchange(): return lax.all_to_all(x, SLAB, split_axis=0, concat_axis=0, tiled=True)  23.4 us
    all_to_all x1, blocking collectives, on_device(): lax.all_to_all(box.reshape(slabs, 4, 128), SLAB, split_axis=0, concat_axi...  23.3 us
    all_to_all x1, blocking collectives, on_device(): lax.all_to_all(copies, ranks, split_axis=0, concat_axis=0, tiled=True)  21.2 us
  transfers between devices with their start and end apart: 4, of which 4 were waited for; matrix products, arithmetic and copies ran while one was open for 0% of the time, Pallas kernels for 33%

profile of v3, /device:TPU:1, one launch (start us, length us, event | category | flops | bytes accessed | tf_op | source)
XLA Modules:
  0.0 304.4 jit_solution(9599547232445304293)
XLA Ops:
  0.6 2.4 pack.1
  3.1 23.3 %all_to_all.30 = f32[64,4,128]{2,1,0:T(4,128)S(1)} all-to-all(f32[64,4,128]{2,1,0:T(4,128)} %bitcast.16), channel_id=1, replica_groups=mesh['chan'=4,'slab_0'=4,'slab_1'=8,'slab_2'=2] {'slab_0','slab_1','slab..., dimensions={0} | all-to-all | bytes 262144 | tf_op jit(solution)/shard_map/all_to_all | solution.py:443
  26.4 0.0 copy-start
  26.4 0.6 shift-right-arithmetic_reduce_fusion.tiles
  27.0 0.0 copy-done
  27.0 14.0 %rows0.1 = (f32[64,64,128]{2,1,0:T(8,128)}, f32[32,64,128]{2,1,0:T(8,128)}) custom-call(s32[128]{0:T(128)} %shift-right-arithmetic_reduce_fusion.tiles, f32[256,128]{1,0:T(8,128)} %bitcast.18, bf16[128,128]{1,0:T(8,128)(2,1)} %constant.37.clone.first_h, f32[2,64,128]{2,1,0:T(8,128)} %constant.38.clone.phases_h, bf16[128,384]{1,0:T(8,128)(2,1)} %constant.39.clone.second_h), custom_call_target="tpu_custom_call" | custom-call | flops 1073741824 | bytes 4194304 | tf_op jit(solution)/shard_map/image/rows0/pallas_call | solution.py:216
  41.0 5.3 %all-to-all-start.3 = ((f32[64,64,128]{2,1,0:T(8,128)}), f32[64,64,128]{2,1,0:T(8,128)}, u32[]{:S(2)}, u32[]{:S(2)}) async-start(f32[64,64,128]{2,1,0:T(8,128)} %get-tuple-element.9), calls=%async_computation.3 | async-start | bytes 4194304 | tf_op jit(solution)/shard_map/image/go0/all_to_all | solution.py:436
  46.4 9.4 %rows1.1 = f32[64,64,128]{2,1,0:T(8,128)} custom-call(f32[32,64,128]{2,1,0:T(8,128)} %get-tuple-element.8.raster_h, bf16[128,128]{1,0:T(8,128)(2,1)} %constant.37.clone.first_h, f32[2,64,128]{2,1,0:T(8,128)} %constant.38.clone.phases_h, bf16[128,384]{1,0:T(8,128)(2,1)} %constant.40.clone.second_h), custom_call_target="tpu_custom_call" | custom-call | flops 1073741824 | bytes 4194304 | tf_op jit(solution)/shard_map/image/rows1/pallas_call | solution.py:216
  55.8 41.8 %all-to-all-done.3.refs_0_ = f32[64,64,128]{2,1,0:T(8,128)} async-done(((f32[64,64,128]{2,1,0:T(8,128)}), f32[64,64,128]{2,1,0:T(8,128)}, u32[]{:S(2)}, u32[]{:S(2)}) %all-to-all-start.3) | async-done | bytes 2097184 | tf_op jit(solution)/shard_map/image/go0/all_to_all | solution.py:436
  97.6 6.0 %all-to-all-start.1 = ((f32[64,64,128]{2,1,0:T(8,128)}), f32[64,64,128]{2,1,0:T(8,128)}, u32[]{:S(2)}, u32[]{:S(2)}) async-start(f32[64,64,128]{2,1,0:T(8,128)} %rows1.1), calls=%async_computation.1 | async-start | bytes 4194304 | tf_op jit(solution)/shard_map/image/go1/all_to_all | solution.py:436
  103.6 39.3 %cols0.1 = f32[64,64,128]{2,1,0:T(8,128)} custom-call(f32[64,64,128]{2,1,0:T(8,128)} %all-to-all-done.3.refs_0_, f32[64,128,128]{2,1,0:T(8,128)} %bitcast.10, f32[64,128,128]{2,1,0:T(8,128)} %bitcast.12, bf16[256,256]{1,0:T(8,128)(2,1)} %constant.41.clone.refs_3_, bf16[128,256]{1,0:T(8,128)(2,1)} %constant.42.clone.refs_4_, ...), custom_call_target="tpu_custom_call" | custom-call | flops 3221225472 | bytes 12582912 | tf_op jit(solution)/shard_map/image/cols0/pallas_call | solution.py:332
  143.0 11.8 %all-to-all-done.1.refs_0_ = f32[64,64,128]{2,1,0:T(8,128)} async-done(((f32[64,64,128]{2,1,0:T(8,128)}), f32[64,64,128]{2,1,0:T(8,128)}, u32[]{:S(2)}, u32[]{:S(2)}) %all-to-all-start.1) | async-done | bytes 2097184 | tf_op jit(solution)/shard_map/image/go1/all_to_all | solution.py:436
  154.8 6.0 %all-to-all-start.4 = ((f32[64,64,128]{2,1,0:T(8,128)}), f32[64,64,128]{2,1,0:T(8,128)}, u32[]{:S(2)}, u32[]{:S(2)}) async-start(f32[64,64,128]{2,1,0:T(8,128)} %cols0.1), calls=%async_computation.4 | async-start | bytes 4194304 | tf_op jit(solution)/shard_map/image/come0/all_to_all | solution.py:436
  160.8 39.3 %cols1.1 = f32[64,64,128]{2,1,0:T(8,128)} custom-call(f32[64,64,128]{2,1,0:T(8,128)} %all-to-all-done.1.refs_0_, f32[64,128,128]{2,1,0:T(8,128)} %bitcast.11, f32[64,128,128]{2,1,0:T(8,128)} %bitcast.13, bf16[256,256]{1,0:T(8,128)(2,1)} %constant.41.clone.refs_3_, bf16[128,256]{1,0:T(8,128)(2,1)} %constant.42.clone.refs_4_, ...), custom_call_target="tpu_custom_call" | custom-call | flops 3221225472 | bytes 12582912 | tf_op jit(solution)/shard_map/image/cols1/pallas_call | solution.py:332
  200.1 11.8 %all-to-all-done.4.y_h = f32[64,64,128]{2,1,0:T(8,128)} async-done(((f32[64,64,128]{2,1,0:T(8,128)}), f32[64,64,128]{2,1,0:T(8,128)}, u32[]{:S(2)}, u32[]{:S(2)}) %all-to-all-start.4) | async-done | bytes 2097184 | tf_op jit(solution)/shard_map/image/come0/all_to_all | solution.py:436
  211.9 6.0 %all-to-all-start.2 = ((f32[64,64,128]{2,1,0:T(8,128)}), f32[64,64,128]{2,1,0:T(8,128)}, u32[]{:S(2)}, u32[]{:S(2)}) async-start(f32[64,64,128]{2,1,0:T(8,128)} %cols1.1), calls=%async_computation.2 | async-start | bytes 4194304 | tf_op jit(solution)/shard_map/image/come1/all_to_all | solution.py:436
  218.0 12.2 %back0.1 = (f32[64,4096]{1,0:T(8,128)}, f32[1,128]{1,0:T(1,128)}) custom-call(f32[64,64,128]{2,1,0:T(8,128)} %all-to-all-done.4.y_h, f32[64,4096]{1,0:T(8,128)} %bitcast.15, bf16[256,256]{1,0:T(8,128)(2,1)} %constant.47.clone.first_h, f32[2,128,128]{2,1,0:T(8,128)} %constant.48.clone.phases_h, bf16[32,384]{1,0:T(8,128)(2,1)} %constant.49.clone.second_h), custom_call_target="tpu_custom_call" | custom-call | tf_op jit(solution)/shard_map/image/back0/pallas_call | solution.py:417
  230.2 38.9 %all-to-all-done.2.y_h = f32[64,64,128]{2,1,0:T(8,128)} async-done(((f32[64,64,128]{2,1,0:T(8,128)}), f32[64,64,128]{2,1,0:T(8,128)}, u32[]{:S(2)}, u32[]{:S(2)}) %all-to-all-start.2) | async-done | bytes 2097184 | tf_op jit(solution)/shard_map/image/come1/all_to_all | solution.py:436
  269.1 12.2 %back1.1 = (f32[64,4096]{1,0:T(8,128)}, f32[1,128]{1,0:T(1,128)}) custom-call(f32[64,64,128]{2,1,0:T(8,128)} %all-to-all-done.2.y_h, f32[64,4096]{1,0:T(8,128)} %get-tuple-element.10.base_h, bf16[256,256]{1,0:T(8,128)(2,1)} %constant.50.clone.first_h, f32[2,128,128]{2,1,0:T(8,128)} %constant.48.clone.phases_h, bf16[32,384]{1,0:T(8,128)(2,1)} %constant.49.clone.second_h), custom_call_target="tpu_custom_call" | custom-call | tf_op jit(solution)/shard_map/image/back1/pallas_call | solution.py:417
  281.2 0.7 broadcast_in_dim.13
  282.0 21.2 %all_to_all.31 = f32[256,1,128]{2,1,0:T(1,128)S(1)} all-to-all(f32[256,1,128]{2,1,0:T(1,128)S(1)} %broadcast_in_dim.13), channel_id=1, replica_groups=mesh['chan'=4,'slab_0'=4,'slab_1'=8,'slab_2'=2] {'chan','slab_0','slab_1..., dimensions={0} | all-to-all | bytes 262144 | tf_op jit(solution)/shard_map/all_to_all | solution.py:458
  303.2 0.7 slice_reduce_fusion
  303.9 0.5 multiply_sqrt_fusion
  (1 shorter events, 0.0 us)
Async XLA Ops:
  26.4 0.7 copy-start
  41.0 56.6 %all-to-all-start.3 = ((f32[64,64,128]{2,1,0:T(8,128)}), f32[64,64,128]{2,1,0:T(8,128)}, u32[]{:S(2)}, u32[]{:S(2)}) async-start(f32[64,64,128]{2,1,0:T(8,128)} %get-tuple-element.9), calls=%async_computation.3 | async-start | bytes 4194304 | tf_op jit(solution)/shard_map/image/go0/all_to_all | solution.py:436
  97.6 57.1 %all-to-all-start.1 = ((f32[64,64,128]{2,1,0:T(8,128)}), f32[64,64,128]{2,1,0:T(8,128)}, u32[]{:S(2)}, u32[]{:S(2)}) async-start(f32[64,64,128]{2,1,0:T(8,128)} %rows1.1), calls=%async_computation.1 | async-start | bytes 4194304 | tf_op jit(solution)/shard_map/image/go1/all_to_all | solution.py:436
  154.8 57.1 %all-to-all-start.4 = ((f32[64,64,128]{2,1,0:T(8,128)}), f32[64,64,128]{2,1,0:T(8,128)}, u32[]{:S(2)}, u32[]{:S(2)}) async-start(f32[64,64,128]{2,1,0:T(8,128)} %cols0.1), calls=%async_computation.4 | async-start | bytes 4194304 | tf_op jit(solution)/shard_map/image/come0/all_to_all | solution.py:436
  211.9 57.1 %all-to-all-start.2 = ((f32[64,64,128]{2,1,0:T(8,128)}), f32[64,64,128]{2,1,0:T(8,128)}, u32[]{:S(2)}, u32[]{:S(2)}) async-start(f32[64,64,128]{2,1,0:T(8,128)} %cols1.1), calls=%async_computation.2 | async-start | bytes 4194304 | tf_op jit(solution)/shard_map/image/come1/all_to_all | solution.py:436

commit v4 on v3

--- a/solution.py
+++ b/solution.py
@@ -14,6 +14,7 @@
 BF = jnp.bfloat16
 F32 = jnp.float32
 GRANT = 65280 << 10
+STEP = 32
 NT = (((1,), (1,)), ((), ()))
 NN = (((1,), (0,)), ((), ()))
 
@@ -69,7 +70,7 @@
         box[pl.ds(2 * slot + 1, 1), :] = jnp.where(lane < counts[i], flux[pl.ds(i, 1), :], 0.0)
         return c
 
-    lax.fori_loop(0, blocks, place, 0)
+    lax.fori_loop(0, blocks, place, 0, unroll=4)
 
 
 def pack(owner, tile, counts, offsets, flux, owners):
@@ -87,17 +88,18 @@
 
 def stacked(x):
     high, low = split(x)
-    return jnp.concatenate([high, low, high, low], 0)
-
-
-def wide(x):
-    high, low = split(x)
-    return jnp.concatenate([high, high, low], 1)
-
-
-def beside(x):
-    high, low = split(x)
-    return jnp.concatenate([high, low, high], 1)
+    return jnp.concatenate([high, low, high], 0)
+
+
+def doubled(high, low):
+    upper = np.concatenate([high, high], 1)
+    return np.concatenate([upper, np.concatenate([low, np.zeros_like(low)], 1)], 0)
+
+
+def across(table, x):
+    both = mul(table, jnp.concatenate(split(x), 1), NT)
+    count = both.shape[0] // 2
+    return both[:count] + both[count:]
 
 
 def turned(whole, count, sg):
@@ -121,12 +123,12 @@
     b = np.arange(128)
     c, s = phase(np.outer(k, a), 64)
     high, low = halves(np.concatenate([c, -s], 0))
-    first = np.concatenate([high, high, low, low], 1)
+    first = np.concatenate([high, high, low], 1)
     tc, ts = phase(np.outer(k, b), 8192)
     phases = np.stack([tc, -ts]).astype(np.float32)
     c, s = phase(np.outer(np.arange(half, 128, 2), b), 128)
     high, low = halves(np.concatenate([c, -s], 0))
-    second = np.concatenate([high, high, low], 1)
+    second = doubled(high, low)
     return first, phases, second
 
 
@@ -135,28 +137,38 @@
     row_ids = lax.broadcasted_iota(jnp.int32, (64, 128), 0)
     col_ids = lax.broadcasted_iota(jnp.int32, (128, 128), 0)
 
-    def image(i):
+    none = jnp.zeros((64, 128), F32)
+
+    def spots(i):
         spot = got[pl.ds(2 * i, 1), :].astype(jnp.int32)
         amount = got[pl.ds(2 * i + 1, 1), :]
         high = amount.astype(BF).astype(F32)
-        low = amount - high
         here = row_ids == ((spot >> 7) & 63)
-        left = jnp.concatenate([jnp.where(here, high, 0.0), jnp.where(here, low, 0.0)], 1)
-        there = jnp.where(col_ids == (spot & 127), 1.0, 0.0).astype(BF)
-        return mul(left.astype(BF), jnp.concatenate([there, there], 1), NT)
+        there = jnp.where(col_ids == (spot & 127), 1.0, 0.0)
+        return jnp.where(here, high, 0.0), jnp.where(here, amount - high, 0.0), there
+
+    def images(i):
+        high0, low0, there0 = spots(i)
+        high1, low1, there1 = spots(i + 1)
+        left = [jnp.concatenate(pair, 1) for pair in ((high0, none), (low0, none), (none, high1), (none, low1))]
+        left = jnp.concatenate(left, 0).astype(BF)
+        both = mul(left, jnp.concatenate([there0, there1], 1).astype(BF), NT)
+        return [both[:64] + both[64:128], both[128:192] + both[192:]]
 
     def blocks(n, c):
-        images = [image(8 * n + u) for u in range(8)]
-        for u in range(8):
-            tile = tiles[8 * n + u]
-            raster[tile] = raster[tile] + images[u]
-        return c
-
-    lax.fori_loop(0, got.shape[0] // 16, blocks, 0)
+        parts = []
+        for u in range(16):
+            parts += images(32 * n + 2 * u)
+        for u in range(32):
+            tile = tiles[32 * n + u]
+            raster[tile] = raster[tile] + parts[u]
+        return c
+
+    lax.fori_loop(0, got.shape[0] // 64, blocks, 0)
 
 
 def band(source, target, sems, n):
-    rows = pl.ds(pl.multiple_of(8 * n, 8), 8)
+    rows = pl.ds(pl.multiple_of(STEP * n, STEP), STEP)
     return pltpu.make_async_copy(source.at[:, rows, :], target.at[:, rows, :], sems.at[n])
 
 
@@ -165,23 +177,22 @@
 
     def rows(n, c):
         results = []
-        start = pl.multiple_of(8 * n, 8)
-        lines = jnp.swapaxes(raster[:, pl.ds(start, 8), :], 0, 1)
-        for u in range(4):
-            both = mul(first[...], stacked(jnp.concatenate([lines[2 * u], lines[2 * u + 1]], 1)))
-            parts = []
-            for v in range(2):
-                re = both[:64, 128 * v : 128 * v + 128]
-                im = both[64:, 128 * v : 128 * v + 128]
-                parts += [re * phases[0] - im * phases[1], re * phases[1] + im * phases[0]]
-            whole = mul(second[...], beside(jnp.concatenate(parts, 0)), NT)
-            results += [turned(whole[:, 128 * v : 128 * v + 128], 64, sg) for v in range(2)]
-        out[:, pl.ds(start, 8), :] = jnp.swapaxes(jnp.stack(results), 0, 1)
+        start = pl.multiple_of(STEP * n, STEP)
+        lines = jnp.swapaxes(raster[:, pl.ds(start, STEP), :], 0, 1)
+        whole = mul(first[...], stacked(jnp.concatenate([lines[u] for u in range(STEP)], 1)))
+        parts = []
+        for u in range(STEP):
+            re = whole[:64, 128 * u : 128 * u + 128]
+            im = whole[64:, 128 * u : 128 * u + 128]
+            parts += [re * phases[0] - im * phases[1], re * phases[1] + im * phases[0]]
+        whole = across(second[...], jnp.concatenate(parts, 0))
+        results += [turned(whole[:, 128 * u : 128 * u + 128], 64, sg) for u in range(STEP)]
+        out[:, pl.ds(start, STEP), :] = jnp.swapaxes(jnp.stack(results), 0, 1)
         band(out, out_h, sems, n).start()
         return c
 
-    lax.fori_loop(0, 8, rows, 0)
-    for n in range(8):
+    lax.fori_loop(0, 64 // STEP, rows, 0)
+    for n in range(64 // STEP):
         band(out, out_h, sems, n).wait()
 
 
@@ -241,10 +252,10 @@
     b = np.arange(64)
     c, s = phase(np.outer(k, a), 128)
     high, low = halves(np.concatenate([c, -s], 0))
-    first = np.concatenate([high, high, low, low], 1)
+    first = np.concatenate([high, high, low], 1)
     c, s = phase(np.outer(b, b), 64)
     high, low = halves(np.concatenate([c, s], 0))
-    inner = np.concatenate([high, high, low, low], 1)
+    inner = np.concatenate([high, high, low], 1)
     c, s = np.concatenate([c, c], 1), np.concatenate([-s, -s], 1)
     w = np.stack([c, s]).astype(np.float32)
     c, s = phase(np.outer(k, b), 8192)
@@ -294,7 +305,9 @@
                 s_row = wt[1, pl.ds(k, 1), :]
                 turn = jnp.concatenate([w[0] * c_row - w[1] * s_row, w[0] * s_row + w[1] * c_row], 0)
                 value = stacked(lines[2 * u + v])
-                spec = turned(mul(jnp.concatenate(split(turn), 1), value), 64, sg)
+                high, low = split(turn)
+                turn = jnp.concatenate([high, low[:, :64]], 1)
+                spec = turned(mul(turn, value), 64, sg)
                 fr = frs[2 * u + v]
                 fi = fis[2 * u + v]
                 fr = jnp.where(own, fr, swap(fr))
@@ -351,12 +364,12 @@
     j = np.arange(half, 128, 2)
     c, s = phase(np.outer(b, j), 128)
     high, low = halves(np.concatenate([c, s], 0))
-    first = np.concatenate([high, high, low, low], 1)
+    first = np.concatenate([high, high, low], 1)
     tc, ts = phase(np.outer(b, k), 8192)
     phases = np.stack([np.concatenate([tc, tc], 1), np.concatenate([-ts, ts], 1)])
     c, s = phase(np.outer(a, k), 64)
     high, low = halves(np.concatenate([c, -s], 1) / (8192.0 * 8192.0))
-    second = np.concatenate([high, high, low], 1)
+    second = doubled(high, low)
     return first, phases.astype(np.float32), second
 
 
@@ -364,7 +377,7 @@
     y_h, base_h, first_h, phases_h, second_h, out_h, stats, image, base, first, phases, second, y, sems, bands, ends
 ):
     copies = fetch([(first_h, first), (phases_h, phases), (second_h, second)], sems)
-    for n in range(8):
+    for n in range(64 // STEP):
         band(y_h, y, bands, n).start()
     keep = pltpu.make_async_copy(base_h, base, sems.at[3])
     keep.start()
@@ -375,20 +388,19 @@
     def rows(n, c):
         results = []
         band(y_h, y, bands, n).wait()
-        start = pl.multiple_of(8 * n, 8)
-        lines = jnp.swapaxes(y[:, pl.ds(start, 8), :], 0, 1)
-        for u in range(4):
-            both = mul(first[...], stacked(jnp.concatenate([lines[2 * u], lines[2 * u + 1]], 1)))
-            parts = []
-            for v in range(2):
-                part = turned(both[:, 128 * v : 128 * v + 128], 128, sg)
-                parts.append(part * phases[0] + swap(part) * phases[1])
-            pair = mul(second[...], beside(jnp.concatenate(parts, 0)), NT)
-            results += [pair[:, :128], pair[:, 128:]]
-        image[:, pl.ds(start, 8), :] = jnp.swapaxes(jnp.stack(results), 0, 1)
-        return c
-
-    lax.fori_loop(0, 8, rows, 0)
+        start = pl.multiple_of(STEP * n, STEP)
+        lines = jnp.swapaxes(y[:, pl.ds(start, STEP), :], 0, 1)
+        whole = mul(first[...], stacked(jnp.concatenate([lines[u] for u in range(STEP)], 1)))
+        parts = []
+        for u in range(STEP):
+            part = turned(whole[:, 128 * u : 128 * u + 128], 128, sg)
+            parts.append(part * phases[0] + swap(part) * phases[1])
+        whole = across(second[...], jnp.concatenate(parts, 0))
+        results += [whole[:, 128 * u : 128 * u + 128] for u in range(STEP)]
+        image[:, pl.ds(start, STEP), :] = jnp.swapaxes(jnp.stack(results), 0, 1)
+        return c
+
+    lax.fori_loop(0, 64 // STEP, rows, 0)
     keep.wait()
     total = jnp.zeros((64, 128), F32)
     top = jnp.zeros((64, 128), F32)

time: 305 us -> 294 us (0.964)
  Pallas kernels: 129 us -> 108 us
  waiting for transfers between devices: 104 us -> 114 us
    pallas_call x2, Pallas kernels: 23.4 us -> 13 us  [rows_call(): pl.pallas_call(body, out_shape=(piece, image) if with_raster else piece,...]
    all_to_all x4, waiting for transfers between devices: 104 us -> 114 us  [exchange(): return lax.all_to_all(x, SLAB, split_axis=0, concat_axis=0, tiled=True)]
    pallas_call x2, Pallas kernels: 24.4 us -> 14.7 us  [backward_rows(): pl.pallas_call(back_body, out_shape=(jax.ShapeDtypeStruct(base.shape, F32...]
  transfers between devices with their start and end apart: 4 -> 4, of which waited for: 4 -> 4; matrix products, arithmetic and copies ran while one was open for 0% -> 0% of each run, Pallas kernels for 33% -> 31%
where the time goes in v4:
time: 294 us; the launch traced here: 293 us
  waiting for transfers between devices  114 us (39%)
  Pallas kernels  108 us (37%)
  blocking collectives  44.5 us (15%)
  starting transfers between devices  23.6 us (8%)
    all_to_all x4, waiting for transfers between devices, exchange(): return lax.all_to_all(x, SLAB, split_axis=0, concat_axis=0, tiled=True)  114 us
    pallas_call x2, Pallas kernels, columns(): pl.pallas_call(lambda *refs: cols_body(half, *refs), out_shape=jax.ShapeD...  77.6 us
    all_to_all x4, starting transfers between devices, exchange(): return lax.all_to_all(x, SLAB, split_axis=0, concat_axis=0, tiled=True)  23.6 us
    all_to_all x1, blocking collectives, on_device(): lax.all_to_all(box.reshape(slabs, 4, 128), SLAB, split_axis=0, concat_axi...  23.3 us
    all_to_all x1, blocking collectives, on_device(): lax.all_to_all(copies, ranks, split_axis=0, concat_axis=0, tiled=True)  21.2 us
    pallas_call x2, Pallas kernels, backward_rows(): pl.pallas_call(back_body, out_shape=(jax.ShapeDtypeStruct(base.shape, F32...  14.7 us
    pallas_call x2, Pallas kernels, rows_call(): pl.pallas_call(body, out_shape=(piece, image) if with_raster else piece,...  13 us
  transfers between devices with their start and end apart: 4, of which 4 were waited for; matrix products, arithmetic and copies ran while one was open for 0% of the time, Pallas kernels for 31%

profile of v4, /device:TPU:1, one launch (start us, length us, event | category | flops | bytes accessed | tf_op | source)
XLA Modules:
  0.0 293.2 jit_solution(6388476264730652257)
XLA Ops:
  0.6 2.2 pack.1
  2.8 23.3 %all_to_all.30 = f32[64,4,128]{2,1,0:T(4,128)S(1)} all-to-all(f32[64,4,128]{2,1,0:T(4,128)} %bitcast.16), channel_id=1, replica_groups=mesh['chan'=4,'slab_0'=4,'slab_1'=8,'slab_2'=2] {'slab_0','slab_1','slab..., dimensions={0} | all-to-all | bytes 262144 | tf_op jit(solution)/shard_map/all_to_all | solution.py:455
  26.1 0.0 copy-start
  26.2 0.6 shift-right-arithmetic_reduce_fusion.tiles
  26.8 0.0 copy-done
  26.8 7.7 %rows0.1 = (f32[64,64,128]{2,1,0:T(8,128)}, f32[32,64,128]{2,1,0:T(8,128)}) custom-call(s32[128]{0:T(128)} %shift-right-arithmetic_reduce_fusion.tiles, f32[256,128]{1,0:T(8,128)} %bitcast.18, bf16[128,96]{1,0:T(8,128)(2,1)} %constant.37.clone.first_h, f32[2,64,128]{2,1,0:T(8,128)} %constant.38.clone.phases_h, bf16[256,256]{1,0:T(8,128)(2,1)} %constant.39.clone.second_h), custom_call_target="tpu_custom_call" | custom-call | flops 1073741824 | bytes 4194304 | tf_op jit(solution)/shard_map/image/rows0/pallas_call | solution.py:227
  34.5 5.3 %all-to-all-start.3 = ((f32[64,64,128]{2,1,0:T(8,128)}), f32[64,64,128]{2,1,0:T(8,128)}, u32[]{:S(2)}, u32[]{:S(2)}) async-start(f32[64,64,128]{2,1,0:T(8,128)} %get-tuple-element.9), calls=%async_computation.3 | async-start | bytes 4194304 | tf_op jit(solution)/shard_map/image/go0/all_to_all | solution.py:448
  39.9 5.3 %rows1.1 = f32[64,64,128]{2,1,0:T(8,128)} custom-call(f32[32,64,128]{2,1,0:T(8,128)} %get-tuple-element.8.raster_h, bf16[128,96]{1,0:T(8,128)(2,1)} %constant.37.clone.first_h, f32[2,64,128]{2,1,0:T(8,128)} %constant.38.clone.phases_h, bf16[256,256]{1,0:T(8,128)(2,1)} %constant.40.clone.second_h), custom_call_target="tpu_custom_call" | custom-call | flops 1073741824 | bytes 4194304 | tf_op jit(solution)/shard_map/image/rows1/pallas_call | solution.py:227
  45.2 45.9 %all-to-all-done.3.refs_0_ = f32[64,64,128]{2,1,0:T(8,128)} async-done(((f32[64,64,128]{2,1,0:T(8,128)}), f32[64,64,128]{2,1,0:T(8,128)}, u32[]{:S(2)}, u32[]{:S(2)}) %all-to-all-start.3) | async-done | bytes 2097184 | tf_op jit(solution)/shard_map/image/go0/all_to_all | solution.py:448
  91.1 6.0 %all-to-all-start.1 = ((f32[64,64,128]{2,1,0:T(8,128)}), f32[64,64,128]{2,1,0:T(8,128)}, u32[]{:S(2)}, u32[]{:S(2)}) async-start(f32[64,64,128]{2,1,0:T(8,128)} %rows1.1), calls=%async_computation.1 | async-start | bytes 4194304 | tf_op jit(solution)/shard_map/image/go1/all_to_all | solution.py:448
  97.1 38.8 %cols0.1 = f32[64,64,128]{2,1,0:T(8,128)} custom-call(f32[64,64,128]{2,1,0:T(8,128)} %all-to-all-done.3.refs_0_, f32[64,128,128]{2,1,0:T(8,128)} %bitcast.10, f32[64,128,128]{2,1,0:T(8,128)} %bitcast.12, bf16[256,192]{1,0:T(8,128)(2,1)} %constant.41.clone.refs_3_, bf16[128,192]{1,0:T(8,128)(2,1)} %constant.42.clone.refs_4_, ...), custom_call_target="tpu_custom_call" | custom-call | flops 3221225472 | bytes 12582912 | tf_op jit(solution)/shard_map/image/cols0/pallas_call | solution.py:345
  136.0 12.3 %all-to-all-done.1.refs_0_ = f32[64,64,128]{2,1,0:T(8,128)} async-done(((f32[64,64,128]{2,1,0:T(8,128)}), f32[64,64,128]{2,1,0:T(8,128)}, u32[]{:S(2)}, u32[]{:S(2)}) %all-to-all-start.1) | async-done | bytes 2097184 | tf_op jit(solution)/shard_map/image/go1/all_to_all | solution.py:448
  148.3 6.0 %all-to-all-start.4 = ((f32[64,64,128]{2,1,0:T(8,128)}), f32[64,64,128]{2,1,0:T(8,128)}, u32[]{:S(2)}, u32[]{:S(2)}) async-start(f32[64,64,128]{2,1,0:T(8,128)} %cols0.1), calls=%async_computation.4 | async-start | bytes 4194304 | tf_op jit(solution)/shard_map/image/come0/all_to_all | solution.py:448
  154.3 38.8 %cols1.1 = f32[64,64,128]{2,1,0:T(8,128)} custom-call(f32[64,64,128]{2,1,0:T(8,128)} %all-to-all-done.1.refs_0_, f32[64,128,128]{2,1,0:T(8,128)} %bitcast.11, f32[64,128,128]{2,1,0:T(8,128)} %bitcast.13, bf16[256,192]{1,0:T(8,128)(2,1)} %constant.41.clone.refs_3_, bf16[128,192]{1,0:T(8,128)(2,1)} %constant.42.clone.refs_4_, ...), custom_call_target="tpu_custom_call" | custom-call | flops 3221225472 | bytes 12582912 | tf_op jit(solution)/shard_map/image/cols1/pallas_call | solution.py:345
  193.1 12.3 %all-to-all-done.4.y_h = f32[64,64,128]{2,1,0:T(8,128)} async-done(((f32[64,64,128]{2,1,0:T(8,128)}), f32[64,64,128]{2,1,0:T(8,128)}, u32[]{:S(2)}, u32[]{:S(2)}) %all-to-all-start.4) | async-done | bytes 2097184 | tf_op jit(solution)/shard_map/image/come0/all_to_all | solution.py:448
  205.4 6.2 %all-to-all-start.2 = ((f32[64,64,128]{2,1,0:T(8,128)}), f32[64,64,128]{2,1,0:T(8,128)}, u32[]{:S(2)}, u32[]{:S(2)}) async-start(f32[64,64,128]{2,1,0:T(8,128)} %cols1.1), calls=%async_computation.2 | async-start | bytes 4194304 | tf_op jit(solution)/shard_map/image/come1/all_to_all | solution.py:448
  211.6 7.4 %back0.1 = (f32[64,4096]{1,0:T(8,128)}, f32[1,128]{1,0:T(1,128)}) custom-call(f32[64,64,128]{2,1,0:T(8,128)} %all-to-all-done.4.y_h, f32[64,4096]{1,0:T(8,128)} %bitcast.15, bf16[256,192]{1,0:T(8,128)(2,1)} %constant.47.clone.first_h, f32[2,128,128]{2,1,0:T(8,128)} %constant.48.clone.phases_h, bf16[64,256]{1,0:T(8,128)(2,1)} %constant.49.clone.second_h), custom_call_target="tpu_custom_call" | custom-call | tf_op jit(solution)/shard_map/image/back0/pallas_call | solution.py:429
  219.0 43.7 %all-to-all-done.2.y_h = f32[64,64,128]{2,1,0:T(8,128)} async-done(((f32[64,64,128]{2,1,0:T(8,128)}), f32[64,64,128]{2,1,0:T(8,128)}, u32[]{:S(2)}, u32[]{:S(2)}) %all-to-all-start.2) | async-done | bytes 2097184 | tf_op jit(solution)/shard_map/image/come1/all_to_all | solution.py:448
  262.7 7.3 %back1.1 = (f32[64,4096]{1,0:T(8,128)}, f32[1,128]{1,0:T(1,128)}) custom-call(f32[64,64,128]{2,1,0:T(8,128)} %all-to-all-done.2.y_h, f32[64,4096]{1,0:T(8,128)} %get-tuple-element.10.base_h, bf16[256,192]{1,0:T(8,128)(2,1)} %constant.50.clone.first_h, f32[2,128,128]{2,1,0:T(8,128)} %constant.48.clone.phases_h, bf16[64,256]{1,0:T(8,128)(2,1)} %constant.49.clone.second_h), custom_call_target="tpu_custom_call" | custom-call | tf_op jit(solution)/shard_map/image/back1/pallas_call | solution.py:429
  270.1 0.7 broadcast_in_dim.13
  270.8 21.2 %all_to_all.31 = f32[256,1,128]{2,1,0:T(1,128)S(1)} all-to-all(f32[256,1,128]{2,1,0:T(1,128)S(1)} %broadcast_in_dim.13), channel_id=1, replica_groups=mesh['chan'=4,'slab_0'=4,'slab_1'=8,'slab_2'=2] {'chan','slab_0','slab_1..., dimensions={0} | all-to-all | bytes 262144 | tf_op jit(solution)/shard_map/all_to_all | solution.py:470
  292.0 0.7 slice_reduce_fusion
  292.7 0.5 multiply_sqrt_fusion
  (1 shorter events, 0.0 us)
Async XLA Ops:
  26.1 0.7 copy-start
  34.5 56.6 %all-to-all-start.3 = ((f32[64,64,128]{2,1,0:T(8,128)}), f32[64,64,128]{2,1,0:T(8,128)}, u32[]{:S(2)}, u32[]{:S(2)}) async-start(f32[64,64,128]{2,1,0:T(8,128)} %get-tuple-element.9), calls=%async_computation.3 | async-start | bytes 4194304 | tf_op jit(solution)/shard_map/image/go0/all_to_all | solution.py:448
  91.1 57.1 %all-to-all-start.1 = ((f32[64,64,128]{2,1,0:T(8,128)}), f32[64,64,128]{2,1,0:T(8,128)}, u32[]{:S(2)}, u32[]{:S(2)}) async-start(f32[64,64,128]{2,1,0:T(8,128)} %rows1.1), calls=%async_computation.1 | async-start | bytes 4194304 | tf_op jit(solution)/shard_map/image/go1/all_to_all | solution.py:448
  148.3 57.1 %all-to-all-start.4 = ((f32[64,64,128]{2,1,0:T(8,128)}), f32[64,64,128]{2,1,0:T(8,128)}, u32[]{:S(2)}, u32[]{:S(2)}) async-start(f32[64,64,128]{2,1,0:T(8,128)} %cols0.1), calls=%async_computation.4 | async-start | bytes 4194304 | tf_op jit(solution)/shard_map/image/come0/all_to_all | solution.py:448
  205.4 57.3 %all-to-all-start.2 = ((f32[64,64,128]{2,1,0:T(8,128)}), f32[64,64,128]{2,1,0:T(8,128)}, u32[]{:S(2)}, u32[]{:S(2)}) async-start(f32[64,64,128]{2,1,0:T(8,128)} %cols1.1), calls=%async_computation.2 | async-start | bytes 4194304 | tf_op jit(solution)/shard_map/image/come1/all_to_all | solution.py:448

commit v5 on v4

--- a/solution.py
+++ b/solution.py
@@ -416,13 +416,13 @@
         saves[-1].start()
     total = jnp.sum(jnp.sum(total, axis=0, keepdims=True), axis=1, keepdims=True)
     top = jnp.max(jnp.max(top, axis=0, keepdims=True), axis=1, keepdims=True)
-    where = lax.broadcasted_iota(jnp.int32, stats.shape, 1)
-    stats[...] = jnp.where(where == 0, total, top)
+    where = lax.broadcasted_iota(jnp.int32, (1, 128), 1)
+    stats[...] = jnp.broadcast_to(jnp.where(where == 0, total, top)[None], stats.shape)
     for save in saves:
         save.wait()
 
 
-def backward_rows(half, y, base):
+def backward_rows(half, y, base, ranks):
     vmem = pl.BlockSpec(memory_space=pltpu.VMEM)
     hbm = pl.BlockSpec(memory_space=pltpu.HBM)
     tables = [jnp.asarray(t) for t in back_tables(half)]
@@ -430,7 +430,7 @@
         back_body,
         out_shape=(
             jax.ShapeDtypeStruct(base.shape, F32),
-            jax.ShapeDtypeStruct((1, 128), F32),
+            jax.ShapeDtypeStruct((ranks, 1, 128), F32),
         ),
         in_specs=[hbm] * (2 + len(tables)),
         out_specs=(hbm, vmem),
@@ -450,6 +450,7 @@
 
 def on_device(flux, offsets, counts, dest_owner, dest_tile, dirty, psf_real, psf_imag):
     slabs = lax.axis_size(SLAB)
+    ranks = ("chan",) + SLAB
     rows_dev, width = dirty.shape[1:]
     box = pack(dest_owner[:, 0], dest_tile, counts, offsets, flux[0], slabs)
     got = lax.all_to_all(
@@ -463,11 +464,9 @@
         arrived1 = exchange(sent[1], "go1")
         back0 = exchange(columns(0, arrived0, *psf), "come0")
         back1 = exchange(columns(1, arrived1, *psf), "come1")
-        partial, _ = backward_rows(0, back0, dirty[0])
-        residual, stats = backward_rows(1, back1, partial)
-    ranks = ("chan",) + SLAB
-    copies = jnp.broadcast_to(stats[:, None, :], (lax.axis_size(ranks), 1, 128))
-    figures = lax.all_to_all(copies, ranks, split_axis=0, concat_axis=0, tiled=True)
+        partial, _ = backward_rows(0, back0, dirty[0], 1)
+        residual, stats = backward_rows(1, back1, partial, lax.axis_size(ranks))
+    figures = lax.all_to_all(stats, ranks, split_axis=0, concat_axis=0, tiled=True)
     figures = figures.reshape(-1, slabs, 128)
     rms_values = jnp.sqrt(jnp.sum(figures[:, :, 0], axis=1) / (rows_dev * slabs * width))
     peak_values = jnp.max(figures[:, :, 1], axis=1)

time: 294 us -> 294 us (level)
  no operation moved by 1% of the time
where the time goes in v5:
time: 294 us; the launch traced here: 293 us
  waiting for transfers between devices  114 us (39%)
  Pallas kernels  108 us (37%)
  blocking collectives  44.7 us (15%)
  starting transfers between devices  23.6 us (8%)
    all_to_all x4, waiting for transfers between devices, exchange(): return lax.all_to_all(x, SLAB, split_axis=0, concat_axis=0, tiled=True)  114 us
    pallas_call x2, Pallas kernels, columns(): pl.pallas_call(lambda *refs: cols_body(half, *refs), out_shape=jax.ShapeD...  77.6 us
    all_to_all x4, starting transfers between devices, exchange(): return lax.all_to_all(x, SLAB, split_axis=0, concat_axis=0, tiled=True)  23.6 us
    all_to_all x1, blocking collectives, on_device(): lax.all_to_all(box.reshape(slabs, 4, 128), SLAB, split_axis=0, concat_axi...  23.3 us
    all_to_all x1, blocking collectives, on_device(): lax.all_to_all(stats, ranks, split_axis=0, concat_axis=0, tiled=True)  21.4 us
    pallas_call x2, Pallas kernels, backward_rows(): pl.pallas_call(back_body, out_shape=(jax.ShapeDtypeStruct(base.shape, F32...  14.8 us
    pallas_call x2, Pallas kernels, rows_call(): pl.pallas_call(body, out_shape=(piece, image) if with_raster else piece,...  13 us
  transfers between devices with their start and end apart: 4, of which 4 were waited for; matrix products, arithmetic and copies ran while one was open for 0% of the time, Pallas kernels for 31%

profile of v5, /device:TPU:1, one launch (start us, length us, event | category | flops | bytes accessed | tf_op | source)
XLA Modules:
  0.0 292.8 jit_solution(14959921172371106013)
XLA Ops:
  0.6 2.2 pack.1
  2.8 23.3 %all_to_all.30 = f32[64,4,128]{2,1,0:T(4,128)S(1)} all-to-all(f32[64,4,128]{2,1,0:T(4,128)} %bitcast.15), channel_id=1, replica_groups=mesh['chan'=4,'slab_0'=4,'slab_1'=8,'slab_2'=2] {'slab_0','slab_1','slab..., dimensions={0} | all-to-all | bytes 262144 | tf_op jit(solution)/shard_map/all_to_all | solution.py:456
  26.1 0.0 copy-start
  26.2 0.6 shift-right-arithmetic_reduce_fusion.tiles
  26.8 0.0 copy-done
  26.8 7.7 %rows0.1 = (f32[64,64,128]{2,1,0:T(8,128)}, f32[32,64,128]{2,1,0:T(8,128)}) custom-call(s32[128]{0:T(128)} %shift-right-arithmetic_reduce_fusion.tiles, f32[256,128]{1,0:T(8,128)} %bitcast.17, bf16[128,96]{1,0:T(8,128)(2,1)} %constant.37.clone.first_h, f32[2,64,128]{2,1,0:T(8,128)} %constant.38.clone.phases_h, bf16[256,256]{1,0:T(8,128)(2,1)} %constant.39.clone.second_h), custom_call_target="tpu_custom_call" | custom-call | flops 1073741824 | bytes 4194304 | tf_op jit(solution)/shard_map/image/rows0/pallas_call | solution.py:227
  34.5 5.3 %all-to-all-start.3 = ((f32[64,64,128]{2,1,0:T(8,128)}), f32[64,64,128]{2,1,0:T(8,128)}, u32[]{:S(2)}, u32[]{:S(2)}) async-start(f32[64,64,128]{2,1,0:T(8,128)} %get-tuple-element.9), calls=%async_computation.3 | async-start | bytes 4194304 | tf_op jit(solution)/shard_map/image/go0/all_to_all | solution.py:448
  39.9 5.3 %rows1.1 = f32[64,64,128]{2,1,0:T(8,128)} custom-call(f32[32,64,128]{2,1,0:T(8,128)} %get-tuple-element.8.raster_h, bf16[128,96]{1,0:T(8,128)(2,1)} %constant.37.clone.first_h, f32[2,64,128]{2,1,0:T(8,128)} %constant.38.clone.phases_h, bf16[256,256]{1,0:T(8,128)(2,1)} %constant.40.clone.second_h), custom_call_target="tpu_custom_call" | custom-call | flops 1073741824 | bytes 4194304 | tf_op jit(solution)/shard_map/image/rows1/pallas_call | solution.py:227
  45.2 45.9 %all-to-all-done.3.refs_0_ = f32[64,64,128]{2,1,0:T(8,128)} async-done(((f32[64,64,128]{2,1,0:T(8,128)}), f32[64,64,128]{2,1,0:T(8,128)}, u32[]{:S(2)}, u32[]{:S(2)}) %all-to-all-start.3) | async-done | bytes 2097184 | tf_op jit(solution)/shard_map/image/go0/all_to_all | solution.py:448
  91.1 6.0 %all-to-all-start.1 = ((f32[64,64,128]{2,1,0:T(8,128)}), f32[64,64,128]{2,1,0:T(8,128)}, u32[]{:S(2)}, u32[]{:S(2)}) async-start(f32[64,64,128]{2,1,0:T(8,128)} %rows1.1), calls=%async_computation.1 | async-start | bytes 4194304 | tf_op jit(solution)/shard_map/image/go1/all_to_all | solution.py:448
  97.1 38.8 %cols0.1 = f32[64,64,128]{2,1,0:T(8,128)} custom-call(f32[64,64,128]{2,1,0:T(8,128)} %all-to-all-done.3.refs_0_, f32[64,128,128]{2,1,0:T(8,128)} %bitcast.9, f32[64,128,128]{2,1,0:T(8,128)} %bitcast.11, bf16[256,192]{1,0:T(8,128)(2,1)} %constant.41.clone.refs_3_, bf16[128,192]{1,0:T(8,128)(2,1)} %constant.42.clone.refs_4_, ...), custom_call_target="tpu_custom_call" | custom-call | flops 3221225472 | bytes 12582912 | tf_op jit(solution)/shard_map/image/cols0/pallas_call | solution.py:345
  136.0 12.3 %all-to-all-done.1.refs_0_ = f32[64,64,128]{2,1,0:T(8,128)} async-done(((f32[64,64,128]{2,1,0:T(8,128)}), f32[64,64,128]{2,1,0:T(8,128)}, u32[]{:S(2)}, u32[]{:S(2)}) %all-to-all-start.1) | async-done | bytes 2097184 | tf_op jit(solution)/shard_map/image/go1/all_to_all | solution.py:448
  148.3 6.0 %all-to-all-start.4 = ((f32[64,64,128]{2,1,0:T(8,128)}), f32[64,64,128]{2,1,0:T(8,128)}, u32[]{:S(2)}, u32[]{:S(2)}) async-start(f32[64,64,128]{2,1,0:T(8,128)} %cols0.1), calls=%async_computation.4 | async-start | bytes 4194304 | tf_op jit(solution)/shard_map/image/come0/all_to_all | solution.py:448
  154.3 38.8 %cols1.1 = f32[64,64,128]{2,1,0:T(8,128)} custom-call(f32[64,64,128]{2,1,0:T(8,128)} %all-to-all-done.1.refs_0_, f32[64,128,128]{2,1,0:T(8,128)} %bitcast.10, f32[64,128,128]{2,1,0:T(8,128)} %bitcast.12, bf16[256,192]{1,0:T(8,128)(2,1)} %constant.41.clone.refs_3_, bf16[128,192]{1,0:T(8,128)(2,1)} %constant.42.clone.refs_4_, ...), custom_call_target="tpu_custom_call" | custom-call | flops 3221225472 | bytes 12582912 | tf_op jit(solution)/shard_map/image/cols1/pallas_call | solution.py:345
  193.1 12.3 %all-to-all-done.4.y_h = f32[64,64,128]{2,1,0:T(8,128)} async-done(((f32[64,64,128]{2,1,0:T(8,128)}), f32[64,64,128]{2,1,0:T(8,128)}, u32[]{:S(2)}, u32[]{:S(2)}) %all-to-all-start.4) | async-done | bytes 2097184 | tf_op jit(solution)/shard_map/image/come0/all_to_all | solution.py:448
  205.4 6.2 %all-to-all-start.2 = ((f32[64,64,128]{2,1,0:T(8,128)}), f32[64,64,128]{2,1,0:T(8,128)}, u32[]{:S(2)}, u32[]{:S(2)}) async-start(f32[64,64,128]{2,1,0:T(8,128)} %cols1.1), calls=%async_computation.2 | async-start | bytes 4194304 | tf_op jit(solution)/shard_map/image/come1/all_to_all | solution.py:448
  211.6 7.4 %back0.1 = (f32[64,4096]{1,0:T(8,128)}, f32[1,1,128]{2,1,0:T(1,128)}) custom-call(f32[64,64,128]{2,1,0:T(8,128)} %all-to-all-done.4.y_h, f32[64,4096]{1,0:T(8,128)} %bitcast.14, bf16[256,192]{1,0:T(8,128)(2,1)} %constant.47.clone.first_h, f32[2,128,128]{2,1,0:T(8,128)} %constant.48.clone.phases_h, bf16[64,256]{1,0:T(8,128)(2,1)} %constant.49.clone.second_h), custom_call_target="tpu_custom_call" | custom-call | tf_op jit(solution)/shard_map/image/back0/pallas_call | solution.py:429
  219.0 43.7 %all-to-all-done.2.y_h = f32[64,64,128]{2,1,0:T(8,128)} async-done(((f32[64,64,128]{2,1,0:T(8,128)}), f32[64,64,128]{2,1,0:T(8,128)}, u32[]{:S(2)}, u32[]{:S(2)}) %all-to-all-start.2) | async-done | bytes 2097184 | tf_op jit(solution)/shard_map/image/come1/all_to_all | solution.py:448
  262.7 7.4 %back1.1 = (f32[64,4096]{1,0:T(8,128)}, f32[256,1,128]{2,1,0:T(1,128)}) custom-call(f32[64,64,128]{2,1,0:T(8,128)} %all-to-all-done.2.y_h, f32[64,4096]{1,0:T(8,128)} %get-tuple-element.10.base_h, bf16[256,192]{1,0:T(8,128)(2,1)} %constant.50.clone.first_h, f32[2,128,128]{2,1,0:T(8,128)} %constant.48.clone.phases_h, bf16[64,256]{1,0:T(8,128)(2,1)} %constant.49.clone.second_h), custom_call_target="tpu_custom_call" | custom-call | tf_op jit(solution)/shard_map/image/back1/pallas_call | solution.py:429
  270.2 21.4 %all_to_all.31 = f32[256,1,128]{2,1,0:T(1,128)S(1)} all-to-all(f32[256,1,128]{2,1,0:T(1,128)} %get-tuple-element.12), channel_id=1, replica_groups=mesh['chan'=4,'slab_0'=4,'slab_1'=8,'slab_2'=2] {'chan','slab_0','slab_1..., dimensions={0} | all-to-all | bytes 262144 | tf_op jit(solution)/shard_map/all_to_all | solution.py:469
  291.6 0.7 slice_reduce_fusion
  292.3 0.5 multiply_sqrt_fusion
  (1 shorter events, 0.0 us)
Async XLA Ops:
  26.1 0.7 copy-start
  34.5 56.6 %all-to-all-start.3 = ((f32[64,64,128]{2,1,0:T(8,128)}), f32[64,64,128]{2,1,0:T(8,128)}, u32[]{:S(2)}, u32[]{:S(2)}) async-start(f32[64,64,128]{2,1,0:T(8,128)} %get-tuple-element.9), calls=%async_computation.3 | async-start | bytes 4194304 | tf_op jit(solution)/shard_map/image/go0/all_to_all | solution.py:448
  91.1 57.1 %all-to-all-start.1 = ((f32[64,64,128]{2,1,0:T(8,128)}), f32[64,64,128]{2,1,0:T(8,128)}, u32[]{:S(2)}, u32[]{:S(2)}) async-start(f32[64,64,128]{2,1,0:T(8,128)} %rows1.1), calls=%async_computation.1 | async-start | bytes 4194304 | tf_op jit(solution)/shard_map/image/go1/all_to_all | solution.py:448
  148.3 57.1 %all-to-all-start.4 = ((f32[64,64,128]{2,1,0:T(8,128)}), f32[64,64,128]{2,1,0:T(8,128)}, u32[]{:S(2)}, u32[]{:S(2)}) async-start(f32[64,64,128]{2,1,0:T(8,128)} %cols0.1), calls=%async_computation.4 | async-start | bytes 4194304 | tf_op jit(solution)/shard_map/image/come0/all_to_all | solution.py:448
  205.4 57.3 %all-to-all-start.2 = ((f32[64,64,128]{2,1,0:T(8,128)}), f32[64,64,128]{2,1,0:T(8,128)}, u32[]{:S(2)}, u32[]{:S(2)}) async-start(f32[64,64,128]{2,1,0:T(8,128)} %cols1.1), calls=%async_computation.2 | async-start | bytes 4194304 | tf_op jit(solution)/shard_map/image/come1/all_to_all | solution.py:448

commit v6 on v5

--- a/solution.py
+++ b/solution.py
@@ -450,7 +450,7 @@
 
 def on_device(flux, offsets, counts, dest_owner, dest_tile, dirty, psf_real, psf_imag):
     slabs = lax.axis_size(SLAB)
-    ranks = ("chan",) + SLAB
+    ranks = SLAB[::-1] + ("chan",)
     rows_dev, width = dirty.shape[1:]
     box = pack(dest_owner[:, 0], dest_tile, counts, offsets, flux[0], slabs)
     got = lax.all_to_all(
@@ -467,9 +467,9 @@
         partial, _ = backward_rows(0, back0, dirty[0], 1)
         residual, stats = backward_rows(1, back1, partial, lax.axis_size(ranks))
     figures = lax.all_to_all(stats, ranks, split_axis=0, concat_axis=0, tiled=True)
-    figures = figures.reshape(-1, slabs, 128)
-    rms_values = jnp.sqrt(jnp.sum(figures[:, :, 0], axis=1) / (rows_dev * slabs * width))
-    peak_values = jnp.max(figures[:, :, 1], axis=1)
+    figures = figures.reshape(slabs, -1, 128)
+    rms_values = jnp.sqrt(jnp.sum(figures[:, :, 0], axis=0) / (rows_dev * slabs * width))
+    peak_values = jnp.max(figures[:, :, 1], axis=0)
     return residual[None], rms_values, peak_values
 
 

time: 294 us -> 294 us (level)
  no operation moved by 1% of the time
where the time goes in v6:
time: 294 us; the launch traced here: 293 us
  waiting for transfers between devices  114 us (39%)
  Pallas kernels  108 us (37%)
  blocking collectives  45 us (15%)
  starting transfers between devices  23.6 us (8%)
    all_to_all x4, waiting for transfers between devices, exchange(): return lax.all_to_all(x, SLAB, split_axis=0, concat_axis=0, tiled=True)  114 us
    pallas_call x2, Pallas kernels, columns(): pl.pallas_call(lambda *refs: cols_body(half, *refs), out_shape=jax.ShapeD...  77.6 us
    all_to_all x4, starting transfers between devices, exchange(): return lax.all_to_all(x, SLAB, split_axis=0, concat_axis=0, tiled=True)  23.6 us
    all_to_all x1, blocking collectives, on_device(): lax.all_to_all(box.reshape(slabs, 4, 128), SLAB, split_axis=0, concat_axi...  23.3 us
    all_to_all x1, blocking collectives, on_device(): lax.all_to_all(stats, ranks, split_axis=0, concat_axis=0, tiled=True)  21.7 us
    pallas_call x2, Pallas kernels, backward_rows(): pl.pallas_call(back_body, out_shape=(jax.ShapeDtypeStruct(base.shape, F32...  14.8 us
    pallas_call x2, Pallas kernels, rows_call(): pl.pallas_call(body, out_shape=(piece, image) if with_raster else piece,...  13 us
  transfers between devices with their start and end apart: 4, of which 4 were waited for; matrix products, arithmetic and copies ran while one was open for 0% of the time, Pallas kernels for 31%

profile of v6, /device:TPU:1, one launch (start us, length us, event | category | flops | bytes accessed | tf_op | source)
XLA Modules:
  0.0 293.1 jit_solution(2776849774184571423)
XLA Ops:
  0.6 2.2 pack.1
  2.8 23.3 %all_to_all.30 = f32[64,4,128]{2,1,0:T(4,128)S(1)} all-to-all(f32[64,4,128]{2,1,0:T(4,128)} %bitcast.15), channel_id=1, replica_groups=mesh['chan'=4,'slab_0'=4,'slab_1'=8,'slab_2'=2] {'slab_0','slab_1','slab..., dimensions={0} | all-to-all | bytes 262144 | tf_op jit(solution)/shard_map/all_to_all | solution.py:456
  26.1 0.0 copy-start
  26.2 0.6 shift-right-arithmetic_reduce_fusion.tiles
  26.8 0.0 copy-done
  26.8 7.8 %rows0.1 = (f32[64,64,128]{2,1,0:T(8,128)}, f32[32,64,128]{2,1,0:T(8,128)}) custom-call(s32[128]{0:T(128)} %shift-right-arithmetic_reduce_fusion.tiles, f32[256,128]{1,0:T(8,128)} %bitcast.17, bf16[128,96]{1,0:T(8,128)(2,1)} %constant.37.clone.first_h, f32[2,64,128]{2,1,0:T(8,128)} %constant.38.clone.phases_h, bf16[256,256]{1,0:T(8,128)(2,1)} %constant.39.clone.second_h), custom_call_target="tpu_custom_call" | custom-call | flops 1073741824 | bytes 4194304 | tf_op jit(solution)/shard_map/image/rows0/pallas_call | solution.py:227
  34.6 5.3 %all-to-all-start.3 = ((f32[64,64,128]{2,1,0:T(8,128)}), f32[64,64,128]{2,1,0:T(8,128)}, u32[]{:S(2)}, u32[]{:S(2)}) async-start(f32[64,64,128]{2,1,0:T(8,128)} %get-tuple-element.9), calls=%async_computation.3 | async-start | bytes 4194304 | tf_op jit(solution)/shard_map/image/go0/all_to_all | solution.py:448
  39.9 5.3 %rows1.1 = f32[64,64,128]{2,1,0:T(8,128)} custom-call(f32[32,64,128]{2,1,0:T(8,128)} %get-tuple-element.8.raster_h, bf16[128,96]{1,0:T(8,128)(2,1)} %constant.37.clone.first_h, f32[2,64,128]{2,1,0:T(8,128)} %constant.38.clone.phases_h, bf16[256,256]{1,0:T(8,128)(2,1)} %constant.40.clone.second_h), custom_call_target="tpu_custom_call" | custom-call | flops 1073741824 | bytes 4194304 | tf_op jit(solution)/shard_map/image/rows1/pallas_call | solution.py:227
  45.2 45.9 %all-to-all-done.3.refs_0_ = f32[64,64,128]{2,1,0:T(8,128)} async-done(((f32[64,64,128]{2,1,0:T(8,128)}), f32[64,64,128]{2,1,0:T(8,128)}, u32[]{:S(2)}, u32[]{:S(2)}) %all-to-all-start.3) | async-done | bytes 2097184 | tf_op jit(solution)/shard_map/image/go0/all_to_all | solution.py:448
  91.1 6.0 %all-to-all-start.1 = ((f32[64,64,128]{2,1,0:T(8,128)}), f32[64,64,128]{2,1,0:T(8,128)}, u32[]{:S(2)}, u32[]{:S(2)}) async-start(f32[64,64,128]{2,1,0:T(8,128)} %rows1.1), calls=%async_computation.1 | async-start | bytes 4194304 | tf_op jit(solution)/shard_map/image/go1/all_to_all | solution.py:448
  97.1 38.8 %cols0.1 = f32[64,64,128]{2,1,0:T(8,128)} custom-call(f32[64,64,128]{2,1,0:T(8,128)} %all-to-all-done.3.refs_0_, f32[64,128,128]{2,1,0:T(8,128)} %bitcast.9, f32[64,128,128]{2,1,0:T(8,128)} %bitcast.11, bf16[256,192]{1,0:T(8,128)(2,1)} %constant.41.clone.refs_3_, bf16[128,192]{1,0:T(8,128)(2,1)} %constant.42.clone.refs_4_, ...), custom_call_target="tpu_custom_call" | custom-call | flops 3221225472 | bytes 12582912 | tf_op jit(solution)/shard_map/image/cols0/pallas_call | solution.py:345
  136.0 12.3 %all-to-all-done.1.refs_0_ = f32[64,64,128]{2,1,0:T(8,128)} async-done(((f32[64,64,128]{2,1,0:T(8,128)}), f32[64,64,128]{2,1,0:T(8,128)}, u32[]{:S(2)}, u32[]{:S(2)}) %all-to-all-start.1) | async-done | bytes 2097184 | tf_op jit(solution)/shard_map/image/go1/all_to_all | solution.py:448
  148.3 6.0 %all-to-all-start.4 = ((f32[64,64,128]{2,1,0:T(8,128)}), f32[64,64,128]{2,1,0:T(8,128)}, u32[]{:S(2)}, u32[]{:S(2)}) async-start(f32[64,64,128]{2,1,0:T(8,128)} %cols0.1), calls=%async_computation.4 | async-start | bytes 4194304 | tf_op jit(solution)/shard_map/image/come0/all_to_all | solution.py:448
  154.3 38.8 %cols1.1 = f32[64,64,128]{2,1,0:T(8,128)} custom-call(f32[64,64,128]{2,1,0:T(8,128)} %all-to-all-done.1.refs_0_, f32[64,128,128]{2,1,0:T(8,128)} %bitcast.10, f32[64,128,128]{2,1,0:T(8,128)} %bitcast.12, bf16[256,192]{1,0:T(8,128)(2,1)} %constant.41.clone.refs_3_, bf16[128,192]{1,0:T(8,128)(2,1)} %constant.42.clone.refs_4_, ...), custom_call_target="tpu_custom_call" | custom-call | flops 3221225472 | bytes 12582912 | tf_op jit(solution)/shard_map/image/cols1/pallas_call | solution.py:345
  193.1 12.3 %all-to-all-done.4.y_h = f32[64,64,128]{2,1,0:T(8,128)} async-done(((f32[64,64,128]{2,1,0:T(8,128)}), f32[64,64,128]{2,1,0:T(8,128)}, u32[]{:S(2)}, u32[]{:S(2)}) %all-to-all-start.4) | async-done | bytes 2097184 | tf_op jit(solution)/shard_map/image/come0/all_to_all | solution.py:448
  205.4 6.2 %all-to-all-start.2 = ((f32[64,64,128]{2,1,0:T(8,128)}), f32[64,64,128]{2,1,0:T(8,128)}, u32[]{:S(2)}, u32[]{:S(2)}) async-start(f32[64,64,128]{2,1,0:T(8,128)} %cols1.1), calls=%async_computation.2 | async-start | bytes 4194304 | tf_op jit(solution)/shard_map/image/come1/all_to_all | solution.py:448
  211.6 7.4 %back0.1 = (f32[64,4096]{1,0:T(8,128)}, f32[1,1,128]{2,1,0:T(1,128)}) custom-call(f32[64,64,128]{2,1,0:T(8,128)} %all-to-all-done.4.y_h, f32[64,4096]{1,0:T(8,128)} %bitcast.14, bf16[256,192]{1,0:T(8,128)(2,1)} %constant.47.clone.first_h, f32[2,128,128]{2,1,0:T(8,128)} %constant.48.clone.phases_h, bf16[64,256]{1,0:T(8,128)(2,1)} %constant.49.clone.second_h), custom_call_target="tpu_custom_call" | custom-call | tf_op jit(solution)/shard_map/image/back0/pallas_call | solution.py:429
  219.0 43.7 %all-to-all-done.2.y_h = f32[64,64,128]{2,1,0:T(8,128)} async-done(((f32[64,64,128]{2,1,0:T(8,128)}), f32[64,64,128]{2,1,0:T(8,128)}, u32[]{:S(2)}, u32[]{:S(2)}) %all-to-all-start.2) | async-done | bytes 2097184 | tf_op jit(solution)/shard_map/image/come1/all_to_all | solution.py:448
  262.7 7.4 %back1.1 = (f32[64,4096]{1,0:T(8,128)}, f32[256,1,128]{2,1,0:T(1,128)}) custom-call(f32[64,64,128]{2,1,0:T(8,128)} %all-to-all-done.2.y_h, f32[64,4096]{1,0:T(8,128)} %get-tuple-element.10.base_h, bf16[256,192]{1,0:T(8,128)(2,1)} %constant.50.clone.first_h, f32[2,128,128]{2,1,0:T(8,128)} %constant.48.clone.phases_h, bf16[64,256]{1,0:T(8,128)(2,1)} %constant.49.clone.second_h), custom_call_target="tpu_custom_call" | custom-call | tf_op jit(solution)/shard_map/image/back1/pallas_call | solution.py:429
  270.2 21.7 %all_to_all.31 = f32[256,1,128]{2,1,0:T(1,128)S(1)} all-to-all(f32[256,1,128]{2,1,0:T(1,128)} %get-tuple-element.12), channel_id=1, replica_groups=mesh['chan'=4,'slab_0'=4,'slab_1'=8,'slab_2'=2] {'slab_2','slab_1','slab..., dimensions={0} | all-to-all | bytes 262144 | tf_op jit(solution)/shard_map/all_to_all | solution.py:469
  291.8 0.8 slice_reduce_fusion
  292.6 0.5 multiply_sqrt_fusion
  (1 shorter events, 0.0 us)
Async XLA Ops:
  26.1 0.7 copy-start
  34.6 56.6 %all-to-all-start.3 = ((f32[64,64,128]{2,1,0:T(8,128)}), f32[64,64,128]{2,1,0:T(8,128)}, u32[]{:S(2)}, u32[]{:S(2)}) async-start(f32[64,64,128]{2,1,0:T(8,128)} %get-tuple-element.9), calls=%async_computation.3 | async-start | bytes 4194304 | tf_op jit(solution)/shard_map/image/go0/all_to_all | solution.py:448
  91.1 57.1 %all-to-all-start.1 = ((f32[64,64,128]{2,1,0:T(8,128)}), f32[64,64,128]{2,1,0:T(8,128)}, u32[]{:S(2)}, u32[]{:S(2)}) async-start(f32[64,64,128]{2,1,0:T(8,128)} %rows1.1), calls=%async_computation.1 | async-start | bytes 4194304 | tf_op jit(solution)/shard_map/image/go1/all_to_all | solution.py:448
  148.3 57.1 %all-to-all-start.4 = ((f32[64,64,128]{2,1,0:T(8,128)}), f32[64,64,128]{2,1,0:T(8,128)}, u32[]{:S(2)}, u32[]{:S(2)}) async-start(f32[64,64,128]{2,1,0:T(8,128)} %cols0.1), calls=%async_computation.4 | async-start | bytes 4194304 | tf_op jit(solution)/shard_map/image/come0/all_to_all | solution.py:448
  205.4 57.3 %all-to-all-start.2 = ((f32[64,64,128]{2,1,0:T(8,128)}), f32[64,64,128]{2,1,0:T(8,128)}, u32[]{:S(2)}, u32[]{:S(2)}) async-start(f32[64,64,128]{2,1,0:T(8,128)} %cols1.1), calls=%async_computation.2 | async-start | bytes 4194304 | tf_op jit(solution)/shard_map/image/come1/all_to_all | solution.py:448
